TPU v7x, 32 devices: a whole 2x2x4 slice. The times are simulated.
32 devices in a mesh: gx: 8 (over z, core), gy: 4 (over y, x).
Axes of the slice: x: 2, y: 2, z: 4, core: 2. Of those that a mesh axis runs over, the one named last changes fastest.
Arguments:
- potential: float32 [32, 64, 256], P('gx', 'gy'), may hold values from -0.2 to 1.2
- recovery: float32 [32, 64, 256], P('gx', 'gy'), may hold values from 0 to 1.5
- fiber_angles: float32 [2, 32, 64, 256], P(None, 'gx', 'gy'), may hold values from -3.140625 to 3.140625
- deform: float32 [9, 8192], P(None, ('gx', 'gy')), may hold values from -0.15 to 1.25, as said below
- elem_slot: int32 [8, 16, 64], P('gx', 'gy'), may hold values from 0 to 8191, as said below
Outputs:
- potential_next: float32 [32, 64, 256], P('gx', 'gy')
- recovery_next: float32 [32, 64, 256], P('gx', 'gy')
Inputs may be any that keep to these rules, and one draw needn't show every extreme that they name: `elem_slot`: entries are distinct. Slot s lies on device s / 256 (rounded down) of gx+gy. The elements of one device's block along gx and gy lie in the slots of the devices with the same index along gx, exactly 64 of them in each. `deform`: components 0, 4 and 8 (the diagonal of F) lie in 0.8 to 1.25, the other six in -0.15 to 0.15.
All inputs are finite; a program needn't handle non-finite values.
Results may differ from a plain program's by a relative error of at most 0.0003.
Values sent between devices are 32-bit elements; how exact they have to be, the bound alone decides.
A program may use at most 64 MiB of HBM per device.

v0:
```python
import jax
import jax.numpy as jnp
from jax import lax
from jax.sharding import PartitionSpec as P

RATIO = 4


sigma_fiber = 1.0
sigma_cross = 0.3
time_step = 0.1
excite_gain = 8.0
excite_level = 0.15
stretch_gain = 10.0
stretch_reversal = 0.6
recover_rate = 0.5


def padded_2(block, sides, width):
    for axis, dim in sides:
        count = lax.axis_size(axis)
        forward = [(i, i + 1) for i in range(count - 1)]
        backward = [(target, source) for source, target in forward]
        low = lax.ppermute(
            lax.slice_in_dim(block, block.shape[dim] - width, None, axis=dim), axis, forward
        )
        high = lax.ppermute(lax.slice_in_dim(block, 0, width, axis=dim), axis, backward)
        block = jnp.concatenate([low, block, high], axis=dim)
    return block


def refine(padded, dim):
    inner_size = padded.shape[dim] - 2
    lower = lax.slice_in_dim(padded, 0, inner_size, axis=dim)
    middle = lax.slice_in_dim(padded, 1, inner_size + 1, axis=dim)
    upper = lax.slice_in_dim(padded, 2, inner_size + 2, axis=dim)
    pieces = []
    for position in range(RATIO):
        offset = (position + 0.5) / RATIO - 0.5
        weight = abs(offset)
        neighbor = lower if offset < 0 else upper
        pieces.append((1.0 - weight) * middle + weight * neighbor)
    stacked = jnp.stack(pieces, axis=dim + 1)
    new_shape = list(padded.shape)
    new_shape[dim] = inner_size * RATIO
    return stacked.reshape(new_shape)


def refine_wide(padded, dim):
    weight = 0.5 - 0.5 / RATIO
    extent = padded.shape[dim]
    low_rim = (1.0 - weight) * lax.slice_in_dim(padded, 0, 1, axis=dim) + weight * lax.slice_in_dim(
        padded, 1, 2, axis=dim
    )
    high_rim = (1.0 - weight) * lax.slice_in_dim(
        padded, extent - 1, extent, axis=dim
    ) + weight * lax.slice_in_dim(padded, extent - 2, extent - 1, axis=dim)
    return jnp.concatenate([low_rim, refine(padded, dim), high_rim], axis=dim)


def directions(angles):
    azimuth = angles[0]
    elevation = angles[1]
    return jnp.stack(
        [
            jnp.cos(azimuth) * jnp.cos(elevation),
            jnp.sin(azimuth) * jnp.cos(elevation),
            jnp.sin(elevation),
        ]
    )


def tensors(field, fiber):
    entries = [field[number] for number in range(9)]

    def element(row_index, col_index):
        return entries[3 * (row_index % 3) + col_index % 3]

    cofactor = [
        [
            element(row_index + 1, col_index + 1) * element(row_index + 2, col_index + 2)
            - element(row_index + 1, col_index + 2) * element(row_index + 2, col_index + 1)
            for col_index in range(3)
        ]
        for row_index in range(3)
    ]
    determinant = (
        element(0, 0) * cofactor[0][0]
        + element(0, 1) * cofactor[0][1]
        + element(0, 2) * cofactor[0][2]
    )
    inverse = [
        [cofactor[col_index][row_index] / determinant for col_index in range(3)]
        for row_index in range(3)
    ]
    stretched = [
        element(row_index, 0) * fiber[0]
        + element(row_index, 1) * fiber[1]
        + element(row_index, 2) * fiber[2]
        for row_index in range(3)
    ]
    stretch = jnp.sqrt(
        stretched[0] * stretched[0] + stretched[1] * stretched[1] + stretched[2] * stretched[2]
    )
    pulled = [
        inverse[row_index][0] * fiber[0]
        + inverse[row_index][1] * fiber[1]
        + inverse[row_index][2] * fiber[2]
        for row_index in range(3)
    ]
    conduct = []
    for first_index, second_index in ((0, 0), (1, 1), (2, 2), (0, 1), (0, 2), (1, 2)):
        metric = (
            inverse[first_index][0] * inverse[second_index][0]
            + inverse[first_index][1] * inverse[second_index][1]
            + inverse[first_index][2] * inverse[second_index][2]
        )
        conduct.append(
            sigma_cross * metric
            + (sigma_fiber - sigma_cross) * pulled[first_index] * pulled[second_index]
        )
    return (jnp.stack(conduct), stretch)


def close_faces(flux, dim, at_first, at_last):
    extent = flux.shape[dim]
    face_index = lax.broadcasted_iota(jnp.int32, flux.shape, dim)
    closed = (face_index == 0) & at_first | (face_index == extent - 1) & at_last
    return jnp.where(closed, jnp.zeros_like(flux), flux)


def divergence(potential_pad, tensor_pad, first_x, last_x, first_y, last_y):
    grad_x = (potential_pad[2:, :, :] - potential_pad[:-2, :, :]) * 0.5
    grad_y = (potential_pad[:, 2:, :] - potential_pad[:, :-2, :]) * 0.5
    grad_z = (potential_pad[:, :, 2:] - potential_pad[:, :, :-2]) * 0.5

    def face_mean(component, dim):
        inner = tensor_pad[component]
        if dim == 0:
            inner = inner[:, 1:-1, 1:-1]
        elif dim == 1:
            inner = inner[1:-1, :, 1:-1]
        else:
            inner = inner[1:-1, 1:-1, :]
        extent = inner.shape[dim]
        return (
            lax.slice_in_dim(inner, 1, extent, axis=dim)
            + lax.slice_in_dim(inner, 0, extent - 1, axis=dim)
        ) * 0.5

    step_x = potential_pad[1:, 1:-1, 1:-1] - potential_pad[:-1, 1:-1, 1:-1]
    mean_y = (grad_y[1:, :, 1:-1] + grad_y[:-1, :, 1:-1]) * 0.5
    mean_z = (grad_z[1:, 1:-1, :] + grad_z[:-1, 1:-1, :]) * 0.5
    flux_x = face_mean(0, 0) * step_x + face_mean(3, 0) * mean_y + face_mean(4, 0) * mean_z
    flux_x = close_faces(flux_x, 0, first_x, last_x)
    step_y = potential_pad[1:-1, 1:, 1:-1] - potential_pad[1:-1, :-1, 1:-1]
    mean_x = (grad_x[:, 1:, 1:-1] + grad_x[:, :-1, 1:-1]) * 0.5
    mean_z = (grad_z[1:-1, 1:, :] + grad_z[1:-1, :-1, :]) * 0.5
    flux_y = face_mean(3, 1) * mean_x + face_mean(1, 1) * step_y + face_mean(5, 1) * mean_z
    flux_y = close_faces(flux_y, 1, first_y, last_y)
    step_z = potential_pad[1:-1, 1:-1, 1:] - potential_pad[1:-1, 1:-1, :-1]
    mean_x = (grad_x[:, 1:-1, 1:] + grad_x[:, 1:-1, :-1]) * 0.5
    mean_y = (grad_y[1:-1, :, 1:] + grad_y[1:-1, :, :-1]) * 0.5
    flux_z = face_mean(4, 2) * mean_x + face_mean(5, 2) * mean_y + face_mean(2, 2) * step_z
    flux_z = close_faces(flux_z, 2, True, True)
    return (
        flux_x[1:]
        - flux_x[:-1]
        + (flux_y[:, 1:] - flux_y[:, :-1])
        + (flux_z[:, :, 1:] - flux_z[:, :, :-1])
    )


def update(voltage, recovery, divergent, stretch):
    current = (
        excite_gain * voltage * (voltage - excite_level) * (voltage - 1.0) + voltage * recovery
    )
    current = current + stretch_gain * jnp.maximum(stretch - 1.0, 0.0) * (
        voltage - stretch_reversal
    )
    voltage_next = voltage + time_step * (divergent - current)
    recovery_next = recovery + time_step * recover_rate * (
        -recovery - excite_gain * voltage * (voltage - excite_level - 1.0)
    )
    return (voltage_next, recovery_next)


def clamp_rim(extended, dim, at_first, at_last):
    extent = extended.shape[dim]
    low_rim = jnp.where(
        at_first,
        lax.slice_in_dim(extended, 1, 2, axis=dim),
        lax.slice_in_dim(extended, 0, 1, axis=dim),
    )
    high_rim = jnp.where(
        at_last,
        lax.slice_in_dim(extended, extent - 2, extent - 1, axis=dim),
        lax.slice_in_dim(extended, extent - 1, extent, axis=dim),
    )
    return jnp.concatenate(
        [low_rim, lax.slice_in_dim(extended, 1, extent - 1, axis=dim), high_rim], axis=dim
    )


def pad_last(values):
    widths = [(0, 0)] * (values.ndim - 1) + [(1, 1)]
    return jnp.pad(values, widths, mode="edge")


def local(potential, recovery, fiber_angles, deform, elem_slot):
    block_x, block_y, block_z = elem_slot.shape
    components = deform.shape[0]
    held_count = deform.shape[1]
    across = lax.axis_size("gx")
    down_count = lax.axis_size("gy")
    at_first_x = lax.axis_index("gx") == 0
    at_last_x = lax.axis_index("gx") == across - 1
    at_first_y = lax.axis_index("gy") == 0
    at_last_y = lax.axis_index("gy") == down_count - 1
    flat_slots = elem_slot.reshape(-1)
    sort_order = jnp.argsort(flat_slots)
    wanted = (flat_slots[sort_order] % held_count).reshape(down_count, -1)
    asked_slots = lax.all_to_all(wanted, "gy", split_axis=0, concat_axis=0, tiled=True)
    picked = deform[:, asked_slots.reshape(-1)].reshape(components, down_count, -1)
    answered = lax.all_to_all(picked, "gy", split_axis=1, concat_axis=1, tiled=True)
    coarse = jnp.zeros((components, flat_slots.shape[0]), jnp.float32)
    coarse = coarse.at[:, sort_order].set(answered.reshape(components, -1))
    coarse = coarse.reshape(components, block_x, block_y, block_z)
    coarse = padded_2(coarse, (("gx", 1), ("gy", 2)), 1)
    coarse = pad_last(
        clamp_rim(clamp_rim(coarse, 1, at_first_x, at_last_x), 2, at_first_y, at_last_y)
    )
    fine_field = refine(refine_wide(refine_wide(coarse, 1), 2), 3)
    angles_wide = padded_2(fiber_angles, (("gx", 1), ("gy", 2)), 1)
    conduct, stretch = tensors(fine_field, directions(angles_wide))
    stretch = stretch[1:-1, 1:-1]
    tensor_pad = pad_last(conduct)
    neighbors = padded_2(potential, (("gx", 0), ("gy", 1)), 1)
    potential_pad = pad_last(
        clamp_rim(clamp_rim(neighbors, 0, at_first_x, at_last_x), 1, at_first_y, at_last_y)
    )
    divergent = divergence(potential_pad, tensor_pad, at_first_x, at_last_x, at_first_y, at_last_y)
    return update(potential, recovery, divergent, stretch)


def solution(mesh):
    placed = (
        P("gx", "gy", None),
        P("gx", "gy", None),
        P(None, "gx", "gy", None),
        P(None, ("gx", "gy")),
        P("gx", "gy", None),
    )
    return jax.shard_map(
        local,
        mesh=mesh,
        in_specs=placed,
        out_specs=(P("gx", "gy", None), P("gx", "gy", None)),
        check_vma=False,
    )
```

profile of v0, /device:TPU:0, one launch (start us, length us, event | category | flops | bytes accessed | tf_op | source)
XLA Modules:
  0.0 99.9 jit_solution(9463944152631830109)
XLA Ops:
  0.6 0.8 reshape.1500
  1.4 3.2 %sort.17 = (s32[256]{0:T(256)}, s32[256]{0:T(256)S(1)}) sort(s32[256]{0:T(256)S(1)} %reshape.1500, s32[256]{0:T(256)S(1)} %iota.29), dimensions={0}, to_apply=%region_0.0 | sort | flops 2048 | bytes 4096 | tf_op jit(solution)/shard_map/jit(argsort)/sort | solution.py:221
  4.6 1.9 %gather_fusion = s32[256]{0:T(256)S(1)} fusion(s32[256]{0:T(256)S(1)} %reshape.1500, s32[1024]{0:T(1024)S(1)} %pad_clamp_fusion.1), kind=kCustom, calls=%fused_computation | custom fusion | bytes 3072 | tf_op jit(solution)/shard_map/gather | solution.py:222
  6.6 0.6 and_select_fusion
  7.2 5.2 %all-to-all-start = ((s32[4,1,64]{2,1,0:T(1,128)}), s32[4,1,64]{2,1,0:T(1,128)S(1)}, u32[]{:S(2)}, u32[]{:S(2)}) async-start(s32[4,1,64]{2,1,0:T(1,128)} %and_select_fusion), calls=%async_computation | async-start | bytes 4096 | tf_op jit(solution)/shard_map/all_to_all | solution.py:223
  12.4 0.7 fusion.88
  13.1 1.3 %collective-permute-start.9 = (f32[1,16,256]{2,1,0:T(8,128)S(1)}, f32[1,16,256]{2,1,0:T(8,128)S(1)}, u32[]{:S(2)}, u32[]{:S(2)}) collective-permute-start(f32[1,16,256]{2,1,0:T(8,128)S(1)} %get-tuple-element.89), channel_id=1, source_target_pairs={{4,0},{8,4},{12,8},{16,12},{20,16},{24,20},{28,24},{5,1},{9,5},{13... | collective-permute-start | bytes 49160 | tf_op jit(solution)/shard_map/ppermute | solution.py:27
  14.4 3.0 %collective-permute-start.8 = (f32[1,16,256]{2,1,0:T(8,128)S(1)}, f32[1,16,256]{2,1,0:T(8,128)S(1)}, u32[]{:S(2)}, u32[]{:S(2)}) collective-permute-start(f32[1,16,256]{2,1,0:T(8,128)S(1)} %get-tuple-element.90), channel_id=1, source_target_pairs={{0,4},{4,8},{8,12},{12,16},{16,20},{20,24},{24,28},{1,5},{5,9},{9,... | collective-permute-start | bytes 49160 | tf_op jit(solution)/shard_map/ppermute | solution.py:24
  17.5 0.8 fusion.85
  18.2 1.3 %collective-permute-start.5 = (f32[2,1,16,256]{3,2,1,0:T(8,128)S(1)}, f32[2,1,16,256]{3,2,1,0:T(8,128)S(1)}, u32[]{:S(2)}, u32[]{:S(2)}) collective-permute-start(f32[2,1,16,256]{3,2,1,0:T(8,128)S(1)} %get-tuple-element.66), channel_id=1, source_target_pairs={{4,0},{8,4},{12,8},{16,12},{20,16},{24,20},{28,24},{5,1},{9,5},{13... | collective-permute-start | bytes 98312 | tf_op jit(solution)/shard_map/ppermute | solution.py:27
  19.5 3.7 %collective-permute-start.4 = (f32[2,1,16,256]{3,2,1,0:T(8,128)S(1)}, f32[2,1,16,256]{3,2,1,0:T(8,128)S(1)}, u32[]{:S(2)}, u32[]{:S(2)}) collective-permute-start(f32[2,1,16,256]{3,2,1,0:T(8,128)S(1)} %get-tuple-element.67), channel_id=1, source_target_pairs={{0,4},{4,8},{8,12},{12,16},{16,20},{20,24},{24,28},{1,5},{5,9},{9,... | collective-permute-start | bytes 98312 | tf_op jit(solution)/shard_map/ppermute | solution.py:24
  23.3 0.5 fusion.80
  23.8 0.6 and_or_fusion
  24.4 0.8 copy.319
  25.2 0.5 broadcast.309
  25.7 0.7 reduce.3
  26.5 0.7 gather_fusion.1
  27.3 0.7 reshape.1544
  28.0 4.2 %all-to-all-start.1 = ((f32[4,1,576]{2,1,0:T(1,128)}), f32[4,1,576]{2,1,0:T(1,128)S(1)}, u32[]{:S(2)}, u32[]{:S(2)}) async-start(f32[4,1,576]{2,1,0:T(1,128)} %reshape.1544), calls=%async_computation.1 | async-start | bytes 20480 | tf_op jit(solution)/shard_map/all_to_all | solution.py:225
  32.2 0.5 and_or_fusion.1
  32.7 4.2 %all-to-all-done.1 = f32[4,1,576]{2,1,0:T(1,128)S(1)} async-done(((f32[4,1,576]{2,1,0:T(1,128)}), f32[4,1,576]{2,1,0:T(1,128)S(1)}, u32[]{:S(2)}, u32[]{:S(2)}) %all-to-all-start.1) | async-done | bytes 9248 | tf_op jit(solution)/shard_map/all_to_all | solution.py:225
  36.9 0.5 broadcast.310
  37.4 0.7 reduce.4
  38.4 1.2 %scatter_custom_fusion = f32[9,256]{0,1:T(8,128)S(1)} fusion(s32[256]{0:T(256)S(1)} %compare_select_fusion.3, f32[256,9]{1,0:T(8,128)S(1)} %copy.322, f32[]{:T(128)} %constant.31.clone.1), kind=kCustom, calls=%fused_computation.163 | custom fusion | bytes 9220 | tf_op jit(solution)/shard_map/scatter | solution.py:227
  39.7 1.3 %collective-permute-start.1 = (f32[9,1,4,64]{3,2,0,1:T(4,128)S(1)}, f32[9,1,4,64]{3,2,0,1:T(4,128)S(1)}, u32[]{:S(2)}, u32[]{:S(2)}) collective-permute-start(f32[9,1,4,64]{3,2,0,1:T(4,128)S(1)} %copy.323), channel_id=1, source_target_pairs={{4,0},{8,4},{12,8},{16,12},{20,16},{24,20},{28,24},{5,1},{9,5},{13... | collective-permute-start | bytes 27656 | tf_op jit(solution)/shard_map/ppermute | solution.py:27
  41.0 3.0 %collective-permute-start = (f32[9,1,4,64]{3,2,0,1:T(4,128)S(1)}, f32[9,1,4,64]{3,2,0,1:T(4,128)S(1)}, u32[]{:S(2)}, u32[]{:S(2)}) collective-permute-start(f32[9,1,4,64]{3,2,0,1:T(4,128)S(1)} %copy.323), channel_id=1, source_target_pairs={{0,4},{4,8},{8,12},{12,16},{16,20},{20,24},{24,28},{1,5},{5,9},{9,... | collective-permute-start | bytes 27656 | tf_op jit(solution)/shard_map/ppermute | solution.py:24
  44.0 1.5 %multiply_add_fusion.4 = (f32[4,16,256]{2,1,0:T(8,128)}, f32[6,16,256]{2,1,0:T(8,128)S(1)}) fusion(f32[4,16,256]{2,1,0:T(8,128)} %param.6, f32[4,16,256]{2,1,0:T(8,128)} %param.5, f32[6,16,256]{2,1,0:T(8,128)S(1)} %constant_dynamic-update-slice_fusion.5), kind=kLoop, calls=%fused_computation.162 | loop fusion | flops 114688 | bytes 262144 | tf_op jit(solution)/shard_map/add | solution.py:182
  45.6 2.5 %collective-permute-start.10 = (f32[6,1,256]{2,1,0:T(1,128)S(1)}, f32[6,1,256]{2,1,0:T(1,128)S(1)}, u32[]{:S(2)}, u32[]{:S(2)}) collective-permute-start(f32[6,1,256]{2,1,0:T(1,128)S(1)} %get-tuple-element.85), channel_id=1, source_target_pairs={{0,1},{1,2},{2,3},{4,5},{5,6},{6,7},{8,9},{9,10},{10,11},{12,13},{... | collective-permute-start | bytes 18440 | tf_op jit(solution)/shard_map/ppermute | solution.py:24
  48.1 1.3 %collective-permute-start.11 = (f32[6,1,256]{2,1,0:T(1,128)S(1)}, f32[6,1,256]{2,1,0:T(1,128)S(1)}, u32[]{:S(2)}, u32[]{:S(2)}) collective-permute-start(f32[6,1,256]{2,1,0:T(1,128)S(1)} %get-tuple-element.86), channel_id=1, source_target_pairs={{1,0},{2,1},{3,2},{5,4},{6,5},{7,6},{9,8},{10,9},{11,10},{13,12},{... | collective-permute-start | bytes 18440 | tf_op jit(solution)/shard_map/ppermute | solution.py:27
  49.4 4.5 %collective-permute-start.2 = (f32[9,3,1,64]{3,2,0,1:T(1,128)S(1)}, f32[9,3,1,64]{3,2,0,1:T(1,128)S(1)}, u32[]{:S(2)}, u32[]{:S(2)}) collective-permute-start(f32[9,3,1,64]{3,2,0,1:T(1,128)S(1)} %get-tuple-element.91), channel_id=1, source_target_pairs={{0,1},{1,2},{2,3},{4,5},{5,6},{6,7},{8,9},{9,10},{10,11},{12,13},{... | collective-permute-start | bytes 20744 | tf_op jit(solution)/shard_map/ppermute | solution.py:24
  54.0 1.3 %collective-permute-start.3 = (f32[9,3,1,64]{3,2,0,1:T(1,128)S(1)}, f32[9,3,1,64]{3,2,0,1:T(1,128)S(1)}, u32[]{:S(2)}, u32[]{:S(2)}) collective-permute-start(f32[9,3,1,64]{3,2,0,1:T(1,128)S(1)} %get-tuple-element.92), channel_id=1, source_target_pairs={{1,0},{2,1},{3,2},{5,4},{6,5},{7,6},{9,8},{10,9},{11,10},{13,12},{... | collective-permute-start | bytes 20744 | tf_op jit(solution)/shard_map/ppermute | solution.py:27
  56.1 4.0 %collective-permute-done.3 = f32[9,3,1,64]{3,2,0,1:T(1,128)S(1)} collective-permute-done((f32[9,3,1,64]{3,2,0,1:T(1,128)S(1)}, f32[9,3,1,64]{3,2,0,1:T(1,128)S(1)}, u32[]{:S(2)}, u32[]{:S(2)}) %collective-permute-start.3) | collective-permute-done | bytes 6944 | tf_op jit(solution)/shard_map/ppermute | solution.py:27
  61.3 0.4 add_bitcast_fusion.3
  62.0 0.7 copy-done.5
  62.7 0.6 copy.407
  63.4 0.6 copy.408
  64.0 1.3 %collective-permute-start.7 = (f32[2,6,1,256]{3,0,2,1:T(2,128)}, f32[2,6,1,256]{3,0,2,1:T(2,128)}, u32[]{:S(2)}, u32[]{:S(2)}) collective-permute-start(f32[2,6,1,256]{3,0,2,1:T(2,128)} %copy.408), channel_id=1, source_target_pairs={{1,0},{2,1},{3,2},{5,4},{6,5},{7,6},{9,8},{10,9},{11,10},{13,12},{... | collective-permute-start | bytes 36872 | tf_op jit(solution)/shard_map/ppermute | solution.py:27
  65.3 5.9 %collective-permute-start.6 = (f32[2,6,1,256]{3,0,2,1:T(2,128)}, f32[2,6,1,256]{3,0,2,1:T(2,128)}, u32[]{:S(2)}, u32[]{:S(2)}) collective-permute-start(f32[2,6,1,256]{3,0,2,1:T(2,128)} %copy.407), channel_id=1, source_target_pairs={{0,1},{1,2},{2,3},{4,5},{5,6},{6,7},{8,9},{9,10},{10,11},{12,13},{... | collective-permute-start | bytes 36872 | tf_op jit(solution)/shard_map/ppermute | solution.py:24
  71.2 1.1 %fusion.81 = (f32[1,6,18,64,4]{3,2,1,0,4:T(8,128)S(1)}, f32[1,6,18,64,4]{3,2,1,0,4:T(8,128)}, f32[1,6,18,64,4]{3,2,1,0,4:T(8,128)}, f32[1,6,18,64,4]{3,2,1,0,4:T...) fusion(f32[9,6,18,64,4]{3,2,1,0,4:T(8,128)S(1)} %pad_maximum_fusion), kind=kLoop, calls=%fused_computation.217 | loop fusion | bytes 1990656 | tf_op jit(solution)/shard_map/slice | solution.py:74
  73.3 1.3 %copy.354 = f32[1,6,18,64,4]{2,4,3,1,0:T(4,128)S(1)} copy(f32[1,6,18,64,4]{3,2,1,0,4:T(8,128)} %get-tuple-element.28) | data formatting | bytes 221184 | tf_op jit(solution)/shard_map/slice | solution.py:74
  75.2 0.8 copy.409
  75.9 1.3 %copy.350 = f32[1,6,18,64,4]{2,4,3,1,0:T(4,128)S(1)} copy(f32[1,6,18,64,4]{3,2,1,0,4:T(8,128)} %get-tuple-element.29) | data formatting | bytes 221184 | tf_op jit(solution)/shard_map/slice | solution.py:74
  77.5 0.9 copy.395
  78.5 1.3 %copy.346 = f32[1,6,18,64,4]{2,4,3,1,0:T(4,128)S(1)} copy(f32[1,6,18,64,4]{3,2,1,0,4:T(8,128)} %get-tuple-element.30) | data formatting | bytes 221184 | tf_op jit(solution)/shard_map/slice | solution.py:74
  80.0 0.9 copy.391
  81.6 0.9 copy.389
  82.5 0.4 copy.341
  83.4 0.8 copy.412
  84.2 1.3 %copy.340 = f32[1,6,18,64,4]{2,4,3,1,0:T(4,128)S(1)} copy(f32[1,6,18,64,4]{3,2,1,0,4:T(8,128)} %get-tuple-element.33) | data formatting | bytes 221184 | tf_op jit(solution)/shard_map/slice | solution.py:74
  86.0 0.8 copy.410
  86.8 0.4 copy.337
  87.6 0.8 copy.413
  88.4 1.3 %copy.336 = f32[1,6,18,64,4]{2,4,3,1,0:T(4,128)S(1)} copy(f32[1,6,18,64,4]{3,2,1,0,4:T(8,128)} %get-tuple-element.35) | data formatting | bytes 221184 | tf_op jit(solution)/shard_map/slice | solution.py:74
  90.3 0.7 copy.371
  91.0 0.7 copy.370
  91.8 1.0 pad_maximum_fusion.4
  92.7 1.3 %fusion.1 = (f32[6,6,18,256]{3,2,1,0:T(8,128)S(1)}, f32[1,6,18,256]{3,2,1,0:T(8,128)S(1)}, f32[1,6,18,256]{3,2,1,0:T(8,128)S(1)}, f32[1,6,18,256]{3,2,1,0:T(8,12...) fusion(f32[2,6,18,256]{3,2,1,0:T(8,128)S(1)} %pad_maximum_fusio, ...), kind=kLoop, calls=%fused_computation.31 | loop fusion | flops 1078271 | bytes 2543616
  94.0 0.6 fusion.7
  94.6 0.6 fusion.11
  95.3 0.6 fusion.3
  95.8 0.6 fusion.38
  96.4 0.6 fusion.9
  97.2 0.5 pad_maximum_fusion.1
  99.2 0.8 fusion.63
  (114 shorter events, 8.8 us)
Async XLA Ops:
  7.2 18.0 %all-to-all-start = ((s32[4,1,64]{2,1,0:T(1,128)}), s32[4,1,64]{2,1,0:T(1,128)S(1)}, u32[]{:S(2)}, u32[]{:S(2)}) async-start(s32[4,1,64]{2,1,0:T(1,128)} %and_select_fusion), calls=%async_computation | async-start | bytes 4096 | tf_op jit(solution)/shard_map/all_to_all | solution.py:223
  13.1 32.4 %collective-permute-start.9 = (f32[1,16,256]{2,1,0:T(8,128)S(1)}, f32[1,16,256]{2,1,0:T(8,128)S(1)}, u32[]{:S(2)}, u32[]{:S(2)}) collective-permute-start(f32[1,16,256]{2,1,0:T(8,128)S(1)} %get-tuple-element.89), channel_id=1, source_target_pairs={{4,0},{8,4},{12,8},{16,12},{20,16},{24,20},{28,24},{5,1},{9,5},{13... | collective-permute-start | bytes 49160 | tf_op jit(solution)/shard_map/ppermute | solution.py:27
  14.4 26.6 %collective-permute-start.8 = (f32[1,16,256]{2,1,0:T(8,128)S(1)}, f32[1,16,256]{2,1,0:T(8,128)S(1)}, u32[]{:S(2)}, u32[]{:S(2)}) collective-permute-start(f32[1,16,256]{2,1,0:T(8,128)S(1)} %get-tuple-element.90), channel_id=1, source_target_pairs={{0,4},{4,8},{8,12},{12,16},{16,20},{20,24},{24,28},{1,5},{5,9},{9,... | collective-permute-start | bytes 49160 | tf_op jit(solution)/shard_map/ppermute | solution.py:24
  18.2 44.4 %collective-permute-start.5 = (f32[2,1,16,256]{3,2,1,0:T(8,128)S(1)}, f32[2,1,16,256]{3,2,1,0:T(8,128)S(1)}, u32[]{:S(2)}, u32[]{:S(2)}) collective-permute-start(f32[2,1,16,256]{3,2,1,0:T(8,128)S(1)} %get-tuple-element.66), channel_id=1, source_target_pairs={{4,0},{8,4},{12,8},{16,12},{20,16},{24,20},{28,24},{5,1},{9,5},{13... | collective-permute-start | bytes 98312 | tf_op jit(solution)/shard_map/ppermute | solution.py:27
  19.5 42.5 %collective-permute-start.4 = (f32[2,1,16,256]{3,2,1,0:T(8,128)S(1)}, f32[2,1,16,256]{3,2,1,0:T(8,128)S(1)}, u32[]{:S(2)}, u32[]{:S(2)}) collective-permute-start(f32[2,1,16,256]{3,2,1,0:T(8,128)S(1)} %get-tuple-element.67), channel_id=1, source_target_pairs={{0,4},{4,8},{8,12},{12,16},{16,20},{20,24},{24,28},{1,5},{5,9},{9,... | collective-permute-start | bytes 98312 | tf_op jit(solution)/shard_map/ppermute | solution.py:24
  28.0 8.9 %all-to-all-start.1 = ((f32[4,1,576]{2,1,0:T(1,128)}), f32[4,1,576]{2,1,0:T(1,128)S(1)}, u32[]{:S(2)}, u32[]{:S(2)}) async-start(f32[4,1,576]{2,1,0:T(1,128)} %reshape.1544), calls=%async_computation.1 | async-start | bytes 20480 | tf_op jit(solution)/shard_map/all_to_all | solution.py:225
  39.7 8.4 %collective-permute-start.1 = (f32[9,1,4,64]{3,2,0,1:T(4,128)S(1)}, f32[9,1,4,64]{3,2,0,1:T(4,128)S(1)}, u32[]{:S(2)}, u32[]{:S(2)}) collective-permute-start(f32[9,1,4,64]{3,2,0,1:T(4,128)S(1)} %copy.323), channel_id=1, source_target_pairs={{4,0},{8,4},{12,8},{16,12},{20,16},{24,20},{28,24},{5,1},{9,5},{13... | collective-permute-start | bytes 27656 | tf_op jit(solution)/shard_map/ppermute | solution.py:27
  41.0 8.4 %collective-permute-start = (f32[9,1,4,64]{3,2,0,1:T(4,128)S(1)}, f32[9,1,4,64]{3,2,0,1:T(4,128)S(1)}, u32[]{:S(2)}, u32[]{:S(2)}) collective-permute-start(f32[9,1,4,64]{3,2,0,1:T(4,128)S(1)} %copy.323), channel_id=1, source_target_pairs={{0,4},{4,8},{8,12},{12,16},{16,20},{20,24},{24,28},{1,5},{5,9},{9,... | collective-permute-start | bytes 27656 | tf_op jit(solution)/shard_map/ppermute | solution.py:24
  45.6 8.4 %collective-permute-start.10 = (f32[6,1,256]{2,1,0:T(1,128)S(1)}, f32[6,1,256]{2,1,0:T(1,128)S(1)}, u32[]{:S(2)}, u32[]{:S(2)}) collective-permute-start(f32[6,1,256]{2,1,0:T(1,128)S(1)} %get-tuple-element.85), channel_id=1, source_target_pairs={{0,1},{1,2},{2,3},{4,5},{5,6},{6,7},{8,9},{9,10},{10,11},{12,13},{... | collective-permute-start | bytes 18440 | tf_op jit(solution)/shard_map/ppermute | solution.py:24
  48.1 7.2 %collective-permute-start.11 = (f32[6,1,256]{2,1,0:T(1,128)S(1)}, f32[6,1,256]{2,1,0:T(1,128)S(1)}, u32[]{:S(2)}, u32[]{:S(2)}) collective-permute-start(f32[6,1,256]{2,1,0:T(1,128)S(1)} %get-tuple-element.86), channel_id=1, source_target_pairs={{1,0},{2,1},{3,2},{5,4},{6,5},{7,6},{9,8},{10,9},{11,10},{13,12},{... | collective-permute-start | bytes 18440 | tf_op jit(solution)/shard_map/ppermute | solution.py:27
  49.4 6.7 %collective-permute-start.2 = (f32[9,3,1,64]{3,2,0,1:T(1,128)S(1)}, f32[9,3,1,64]{3,2,0,1:T(1,128)S(1)}, u32[]{:S(2)}, u32[]{:S(2)}) collective-permute-start(f32[9,3,1,64]{3,2,0,1:T(1,128)S(1)} %get-tuple-element.91), channel_id=1, source_target_pairs={{0,1},{1,2},{2,3},{4,5},{5,6},{6,7},{8,9},{9,10},{10,11},{12,13},{... | collective-permute-start | bytes 20744 | tf_op jit(solution)/shard_map/ppermute | solution.py:24
  54.0 6.1 %collective-permute-start.3 = (f32[9,3,1,64]{3,2,0,1:T(1,128)S(1)}, f32[9,3,1,64]{3,2,0,1:T(1,128)S(1)}, u32[]{:S(2)}, u32[]{:S(2)}) collective-permute-start(f32[9,3,1,64]{3,2,0,1:T(1,128)S(1)} %get-tuple-element.92), channel_id=1, source_target_pairs={{1,0},{2,1},{3,2},{5,4},{6,5},{7,6},{9,8},{10,9},{11,10},{13,12},{... | collective-permute-start | bytes 20744 | tf_op jit(solution)/shard_map/ppermute | solution.py:27
  61.8 0.9 copy-start.5
  62.7 2.6 %copy-start.4 = (f32[2,6,16,256]{3,2,1,0:T(8,128)}, f32[2,6,16,256]{3,2,1,0:T(8,128)S(1)}, u32[]{:S(2)}) copy-start(f32[2,6,16,256]{3,2,1,0:T(8,128)S(1)} %constant_dynamic-update-slice_fusion) | copy-start | bytes 589828
  64.0 26.3 %collective-permute-start.7 = (f32[2,6,1,256]{3,0,2,1:T(2,128)}, f32[2,6,1,256]{3,0,2,1:T(2,128)}, u32[]{:S(2)}, u32[]{:S(2)}) collective-permute-start(f32[2,6,1,256]{3,0,2,1:T(2,128)} %copy.408), channel_id=1, source_target_pairs={{1,0},{2,1},{3,2},{5,4},{6,5},{7,6},{9,8},{10,9},{11,10},{13,12},{... | collective-permute-start | bytes 36872 | tf_op jit(solution)/shard_map/ppermute | solution.py:27
  65.3 25.7 %collective-permute-start.6 = (f32[2,6,1,256]{3,0,2,1:T(2,128)}, f32[2,6,1,256]{3,0,2,1:T(2,128)}, u32[]{:S(2)}, u32[]{:S(2)}) collective-permute-start(f32[2,6,1,256]{3,0,2,1:T(2,128)} %copy.407), channel_id=1, source_target_pairs={{0,1},{1,2},{2,3},{4,5},{5,6},{6,7},{8,9},{9,10},{10,11},{12,13},{... | collective-permute-start | bytes 36872 | tf_op jit(solution)/shard_map/ppermute | solution.py:24
  97.2 0.8 copy-start.11
  97.8 0.7 copy-start.12
  97.8 1.0 copy-start.13
  97.8 1.2 %copy-start = (f32[6,18,256]{2,1,0:T(8,128)S(1)}, f32[6,18,256]{2,1,0:T(8,128)}, u32[]{:S(2)}) copy-start(f32[6,18,256]{2,1,0:T(8,128)} %copy.395) | copy-start | bytes 331780
  97.8 1.2 %copy-start.1 = (f32[6,18,256]{2,1,0:T(8,128)S(1)}, f32[6,18,256]{2,1,0:T(8,128)}, u32[]{:S(2)}) copy-start(f32[6,18,256]{2,1,0:T(8,128)} %copy.391) | copy-start | bytes 331780
  97.8 1.2 %copy-start.2 = (f32[6,18,256]{2,1,0:T(8,128)S(1)}, f32[6,18,256]{2,1,0:T(8,128)}, u32[]{:S(2)}) copy-start(f32[6,18,256]{2,1,0:T(8,128)} %copy.389) | copy-start | bytes 331780
  97.9 1.2 %copy-start.3 = (f32[4,16,256]{2,1,0:T(8,128)S(1)}, f32[4,16,256]{2,1,0:T(8,128)}, u32[]{:S(2)}) copy-start(f32[4,16,256]{2,1,0:T(8,128)} %param.5) | copy-start | bytes 196612
  97.9 1.2 %copy-start.6 = (f32[4,16,256]{2,1,0:T(8,128)S(1)}, f32[4,16,256]{2,1,0:T(8,128)}, u32[]{:S(2)}) copy-start(f32[4,16,256]{2,1,0:T(8,128)} %copy.409) | copy-start | bytes 196612
  97.9 1.2 %copy-start.7 = (f32[4,16,256]{2,1,0:T(8,128)S(1)}, f32[4,16,256]{2,1,0:T(8,128)}, u32[]{:S(2)}) copy-start(f32[4,16,256]{2,1,0:T(8,128)} %copy.412) | copy-start | bytes 196612
  97.9 1.2 %copy-start.8 = (f32[4,16,256]{2,1,0:T(8,128)S(1)}, f32[4,16,256]{2,1,0:T(8,128)}, u32[]{:S(2)}) copy-start(f32[4,16,256]{2,1,0:T(8,128)} %copy.410) | copy-start | bytes 196612
  97.9 1.2 %copy-start.9 = (f32[4,16,256]{2,1,0:T(8,128)S(1)}, f32[4,16,256]{2,1,0:T(8,128)}, u32[]{:S(2)}) copy-start(f32[4,16,256]{2,1,0:T(8,128)} %copy.413) | copy-start | bytes 196612
  98.0 1.2 %copy-start.10 = (f32[4,16,256]{2,1,0:T(8,128)S(1)}, f32[4,16,256]{2,1,0:T(8,128)}, u32[]{:S(2)}) copy-start(f32[4,16,256]{2,1,0:T(8,128)} %param.6) | copy-start | bytes 196612
where the time goes:
time: 101 us; the launch traced here: 99.9 us
  starting transfers between devices  39.8 us (39%)
  local copies, waits for them, and re-layouts  32.6 us (32%)
  other arithmetic  17.9 us (18%)
  waiting for transfers between devices  8.2 us (8%)
  between operations  1.42 us (1%)
    ppermute x6, starting transfers between devices, padded_2(): lax.ppermute(lax.slice_in_dim(block, block.shape[dim] - width, None, axis...  22.7 us
    slice x10, local copies, waits for them, and re-layouts, tensors(): entries = [field[number] for number in range(9)]  9.17 us
    ppermute x6, starting transfers between devices, padded_2(): lax.ppermute(lax.slice_in_dim(block, 0, width, axis=dim), axis, backward)  7.72 us
    unnamed x41, local copies, waits for them, and re-layouts  7.11 us
    squeeze x13, local copies, waits for them, and re-layouts, tensors(): entries = [field[number] for number in range(9)]  5.44 us
    all_to_all x1, starting transfers between devices, local(): lax.all_to_all(wanted, 'gy', split_axis=0, concat_axis=0, tiled=True)  5.19 us
    all_to_all x1, starting transfers between devices, local(): lax.all_to_all(picked, 'gy', split_axis=1, concat_axis=1, tiled=True)  4.19 us
    all_to_all x1, waiting for transfers between devices, local(): lax.all_to_all(picked, 'gy', split_axis=1, concat_axis=1, tiled=True)  4.19 us
  transfers between devices with their start and end apart: 14, of which 2 were waited for; matrix products, arithmetic and copies ran while one was open for 33% of the time, Pallas kernels for 0%

commit v1 on v0

v1 whole, which is shorter than its diff:
```python
import functools

import jax
import jax.numpy as jnp
from jax import lax
from jax.experimental import pallas as pl
from jax.experimental.pallas import tpu as pltpu
from jax.sharding import PartitionSpec as P

MESH = pl.DeviceIdType.MESH
RATIO = 4
LANES = 128
TOP = 8

SIDES = tuple((dx, dy) for dx in (-1, 0, 1) for dy in (-1, 0, 1) if (dx, dy) != (0, 0))


def split_two(values):
    high = values.astype(jnp.bfloat16)
    low = (values - high.astype(jnp.float32)).astype(jnp.bfloat16)
    return high, low


def dot_two(values, weights):
    high, low = split_two(values)
    return jnp.dot(high, weights, preferred_element_type=jnp.float32) + jnp.dot(
        low, weights, preferred_element_type=jnp.float32
    )


def sine_cosine(angle):
    turn = jnp.floor(angle * 0.6366197723675814 + 0.5)
    rest = angle - turn * 1.5703125
    rest = rest - turn * 4.8375129699707031e-4
    rest = rest - turn * 7.549789948768648e-8
    square = rest * rest
    sine = rest + rest * square * (
        -1.6666654611e-1 + square * (8.3321608736e-3 + square * -1.9515295891e-4)
    )
    cosine = (
        1.0
        - 0.5 * square
        + square
        * square
        * (4.166664568298827e-2 + square * (-1.388731625493765e-3 + square * 2.443315711809948e-5))
    )
    size = jnp.abs(turn)
    odd = size == 1.0
    sine_part = jnp.where(odd, cosine * turn, sine)
    cosine_part = jnp.where(odd, sine * -turn, cosine)
    flip = jnp.where(size == 2.0, -1.0, 1.0)
    return sine_part * flip, cosine_part * flip


def fiber_of(azimuth, elevation):
    sin_u, cos_u = sine_cosine(azimuth)
    sin_e, cos_e = sine_cosine(elevation)
    return cos_u * cos_e, sin_u * cos_e, sin_e


def tensor_of(entries, fiber):
    def element(i, j):
        return entries[3 * (i % 3) + j % 3]

    adjugate = [
        [
            element(j + 1, i + 1) * element(j + 2, i + 2)
            - element(j + 1, i + 2) * element(j + 2, i + 1)
            for j in range(3)
        ]
        for i in range(3)
    ]
    determinant = (
        element(0, 0) * adjugate[0][0]
        + element(0, 1) * adjugate[1][0]
        + element(0, 2) * adjugate[2][0]
    )
    inverse = 1.0 / determinant
    square = inverse * inverse
    cross = 0.3 * square
    along = 0.7 * square
    pulled = [
        adjugate[i][0] * fiber[0] + adjugate[i][1] * fiber[1] + adjugate[i][2] * fiber[2]
        for i in range(3)
    ]
    scaled = [along * pulled[i] for i in range(3)]
    conduct = []
    for i, j in ((0, 0), (1, 1), (2, 2), (0, 1), (0, 2), (1, 2)):
        metric = (
            adjugate[i][0] * adjugate[j][0]
            + adjugate[i][1] * adjugate[j][1]
            + adjugate[i][2] * adjugate[j][2]
        )
        conduct.append(cross * metric + scaled[i] * pulled[j])
    return conduct


def stretch_of(entries, fiber):
    parts = [
        entries[3 * i] * fiber[0] + entries[3 * i + 1] * fiber[1] + entries[3 * i + 2] * fiber[2]
        for i in range(3)
    ]
    return jnp.sqrt(parts[0] * parts[0] + parts[1] * parts[1] + parts[2] * parts[2])


def kernel(
    across,
    down,
    sizes,
    potential,
    recovery,
    angles,
    deform,
    slots,
    next_potential,
    next_recovery,
    volts,
    rest_in,
    own_angles,
    x_angles,
    y_angles,
    held,
    near_slots,
    fibers,
    conducts,
    stretches,
    send_sem,
    deform_sem,
    near_sem,
    local_sem,
):
    bx, by, nz, ex, ey, ez, parts, count = sizes
    gx, gy = lax.axis_index("gx"), lax.axis_index("gy")
    first_x, last_x = gx == 0, gx == across - 1
    first_y, last_y = gy == 0, gy == down - 1

    def exists(dx, dy):
        checks = []
        if dx:
            checks.append(jnp.logical_not(first_x if dx < 0 else last_x))
        if dy:
            checks.append(jnp.logical_not(first_y if dy < 0 else last_y))
        return checks[0] if len(checks) == 1 else jnp.logical_and(*checks)

    barrier = pltpu.get_barrier_semaphore()

    def row_targets(dx):
        for step in range(0 if dx else 1, down):
            yield step, lax.rem(gy + step, down)

    def greet(dx):
        for _, target in row_targets(dx):
            pl.semaphore_signal(barrier, inc=1, device_id=(gx + dx, target), device_id_type=MESH)

    pl.when(exists(-1, 0))(lambda: greet(-1))
    greet(0)
    pl.when(exists(1, 0))(lambda: greet(1))

    own = [
        pltpu.make_async_copy(
            potential, volts.at[pl.ds(1, bx), pl.ds(TOP, by), :], local_sem.at[0]
        ),
        pltpu.make_async_copy(recovery, rest_in, local_sem.at[1]),
        pltpu.make_async_copy(angles, own_angles, local_sem.at[2]),
        pltpu.make_async_copy(deform, held.at[1, gy], local_sem.at[3]),
        pltpu.make_async_copy(slots, near_slots.at[1, 1], local_sem.at[4]),
    ]
    for copy in (own[2], own[4], own[3], own[0], own[1]):
        copy.start()

    rows_here = 1 + jnp.where(first_x, 0, 1) + jnp.where(last_x, 0, 1)
    pl.semaphore_wait(barrier, rows_here * down - 1)

    def deform_copy(dx, step, target):
        index = (1 - dx) * down + step
        return pltpu.make_async_remote_copy(
            src_ref=deform,
            dst_ref=held.at[1 - dx, gy],
            send_sem=send_sem.at[index],
            recv_sem=deform_sem.at[index],
            device_id=(gx + dx, target),
            device_id_type=MESH,
        )

    def near_copies(dx, dy):
        place = (1 - dx) * 3 + (1 - dy)
        base = 3 * down + 3 * place
        x_source = pl.ds(0, bx) if dx == 0 else pl.ds(0 if dx < 0 else bx - 1, 1)
        x_target = pl.ds(1, bx) if dx == 0 else pl.ds(bx + 1 if dx < 0 else 0, 1)
        y_source = pl.ds(0, by) if dy == 0 else pl.ds(0 if dy < 0 else by - 1, 1)
        y_target = pl.ds(TOP, by) if dy == 0 else pl.ds(TOP + by if dy < 0 else TOP - 1, 1)
        pairs = [
            (slots, near_slots.at[1 - dx, 1 - dy]),
            (potential.at[x_source, y_source, :], volts.at[x_target, y_target, :]),
        ]
        if dy == 0:
            pairs.append((angles.at[:, x_source], x_angles.at[:, pl.ds(1 if dx < 0 else 0, 1)]))
        elif dx == 0:
            pairs.append((angles.at[:, :, y_source], y_angles.at[1 if dy < 0 else 0]))
        return [
            pltpu.make_async_remote_copy(
                src_ref=source,
                dst_ref=target,
                send_sem=send_sem.at[base + number],
                recv_sem=near_sem.at[3 * place + number],
                device_id=(gx + dx, gy + dy),
                device_id_type=MESH,
            )
            for number, (source, target) in enumerate(pairs)
        ]

    def over_row(dx, act):
        for step, target in row_targets(dx):
            act(deform_copy(dx, step, target))

    def over_near(dx, dy, act):
        for copy in near_copies(dx, dy):
            act(copy)

    def everything(act, way=1):
        def side(dx, dy):
            pl.when(exists(way * dx, way * dy))(lambda: over_near(dx, dy, act))

        for dx in (-1, 0, 1):
            if dx:
                pl.when(exists(way * dx, 0))(lambda dx=dx: over_row(dx, act))
            else:
                over_row(0, act)
        for dx, dy in SIDES:
            side(dx, dy)

    everything(lambda copy: copy.start())

    width = (ey + 2) * ez
    tall = by + 8
    row = lax.broadcasted_iota(jnp.int32, (tall, width), 0)
    lane = lax.broadcasted_iota(jnp.int32, (tall, width), 1)
    cell = jnp.where(row < by, row, jnp.where(row < by + bx, -1, by))
    spot = (cell.astype(jnp.float32) + 0.5) * (1.0 / RATIO) - 0.5
    weight_y = jnp.maximum(1.0 - jnp.abs(spot - ((lane // ez) - 1).astype(jnp.float32)), 0.0)
    row = lax.broadcasted_iota(jnp.int32, (width, nz), 0)
    lane = lax.broadcasted_iota(jnp.int32, (width, nz), 1)
    spot = jnp.clip((lane.astype(jnp.float32) + 0.5) * (1.0 / RATIO) - 0.5, 0.0, ez - 1.0)
    weight_z = jnp.maximum(1.0 - jnp.abs(spot - lax.rem(row, ez).astype(jnp.float32)), 0.0)
    weight_z = weight_z.astype(jnp.bfloat16)

    own[2].wait()
    for s in range(bx):
        for number, part in enumerate(fiber_of(own_angles[0, s], own_angles[1, s])):
            fibers[number, s + 1] = part

    for number in (4, 3, 0, 1):
        own[number].wait()

    everything(lambda copy: copy.wait_recv(), -1)

    gathered = []
    digits = lax.broadcasted_iota(jnp.int32, (LANES, width), 0)
    blocks = count // LANES
    for q in range(3):
        low = jnp.where(first_y, near_slots[q, 1, 0, 0:1], near_slots[q, 0, 0, ey - 1 : ey])
        high = jnp.where(last_y, near_slots[q, 1, 0, ey - 1 : ey], near_slots[q, 2, 0, 0:1])
        pieces = [low] + [near_slots[q, 1, 0, c : c + 1] for c in range(ey)] + [high]
        index = jnp.concatenate(pieces, axis=1) - (gx + q - 1) * (down * count)
        chosen = (digits == (index & (LANES - 1))).astype(jnp.float32).astype(jnp.bfloat16)
        table = []
        for h in range(down):
            block = held[q, h]
            block = jnp.concatenate([block, jnp.zeros((16 - parts, count), jnp.float32)], axis=0)
            table += [block[:, b * LANES : (b + 1) * LANES] for b in range(blocks)]
        found = dot_two(jnp.concatenate(table, axis=0), chosen)
        page = index >> (LANES.bit_length() - 1)
        total = jnp.zeros((16, width), jnp.float32)
        for h in range(down * blocks):
            total = jnp.where(page == h, found[16 * h : 16 * h + 16], total)
        gathered.append(total)
    gathered[0] = jnp.where(first_x, gathered[1], gathered[0])
    gathered[2] = jnp.where(last_x, gathered[1], gathered[2])

    refined = []
    for q in range(3):
        spread = [weight_y * gathered[q][k : k + 1] for k in range(parts)]
        refined.append(dot_two(jnp.concatenate(spread, axis=0), weight_z))

    @pl.when(first_y)
    def _():
        volts[:, TOP - 1 : TOP] = volts[:, TOP : TOP + 1]

    @pl.when(last_y)
    def _():
        volts[:, TOP + by : TOP + by + 1] = volts[:, TOP + by - 1 : TOP + by]

    @pl.when(first_x)
    def _():
        volts[0] = volts[1]

    @pl.when(last_x)
    def _():
        volts[bx + 1] = volts[bx]

    for side, s in ((0, 0), (1, bx + 1)):
        for number, part in enumerate(fiber_of(x_angles[0, side], x_angles[1, side])):
            fibers[number, s] = part
    rim = [
        jnp.concatenate([y_angles[side, c, s] for side in range(2) for s in range(bx)], axis=0)
        for c in range(2)
    ]
    rim_fiber = fiber_of(rim[0], rim[1])

    def hat(s):
        spot = (s + 0.5) / RATIO - 0.5
        return [max(0.0, 1.0 - abs(spot - (q - 1))) for q in range(3)]

    for s in range(bx + 2):
        weights = hat(s - 1)
        for half in range(by // 8):
            rows = slice(8 * half, 8 * half + 8)
            entries = []
            for k in range(parts):
                at = tall * k + 8 * half
                terms = [w * refined[q][at : at + 8] for q, w in enumerate(weights) if w]
                entries.append(functools.reduce(jnp.add, terms))
            fiber = [fibers[number, s, rows] for number in range(3)]
            for number, value in enumerate(tensor_of(entries, fiber)):
                conducts[number, s, TOP + 8 * half : TOP + 8 * half + 8] = value
            if 1 <= s <= bx:
                stretches[s - 1, rows] = stretch_of(entries, fiber)
    rim_row = lax.rem(lax.broadcasted_iota(jnp.int32, (2 * bx, nz), 0), bx).astype(jnp.float32)
    spot = (rim_row + 0.5) * (1.0 / RATIO) - 0.5
    rim_weights = [jnp.maximum(1.0 - jnp.abs(spot - (q - 1.0)), 0.0) for q in range(3)]
    entries = []
    for k in range(parts):
        at = tall * k + by
        entries.append(
            functools.reduce(
                jnp.add, [rim_weights[q] * refined[q][at : at + 2 * bx] for q in range(3)]
            )
        )
    for number, value in enumerate(tensor_of(entries, rim_fiber)):
        for s in range(bx):
            conducts[number, s + 1, TOP - 1 : TOP] = value[s : s + 1]
            conducts[number, s + 1, TOP + by : TOP + by + 1] = value[bx + s : bx + s + 1]

    z_lane = lax.broadcasted_iota(jnp.int32, (by, nz), 1)
    y_row = lax.broadcasted_iota(jnp.int32, (by, nz), 0)

    def next_z(values):
        return jnp.where(z_lane == nz - 1, values, pltpu.roll(values, nz - 1, 1))

    def last_z(values):
        return jnp.where(z_lane == 0, values, pltpu.roll(values, 1, 1))

    def grad_z(values):
        return next_z(values) - last_z(values)

    def at(s, shift):
        return volts[s, TOP + shift : TOP + shift + by]

    def tensor(number, s, shift=0):
        return conducts[number, s, TOP + shift : TOP + shift + by]

    XX, YY, ZZ, XY, XZ, YZ = range(6)
    middle = [at(s, 0) for s in range(bx + 2)]
    grads_y = [at(s, 1) - at(s, -1) for s in range(bx + 2)]
    grads_z = [grad_z(middle[s]) for s in range(bx + 2)]

    def face_x(f):
        def mean(number):
            return tensor(number, f) + tensor(number, f + 1)

        return (
            0.5 * mean(XX) * (middle[f + 1] - middle[f])
            + 0.125 * mean(XY) * (grads_y[f] + grads_y[f + 1])
            + 0.125 * mean(XZ) * (grads_z[f] + grads_z[f + 1])
        )

    faces = [face_x(f) for f in range(bx + 1)]
    faces[0] = jnp.where(first_x, 0.0, faces[0])
    faces[bx] = jnp.where(last_x, 0.0, faces[bx])

    for i in range(bx):
        s = i + 1
        grad_x = middle[s + 1] - middle[s - 1]

        def face_y(shift):
            def mean(number):
                return tensor(number, s) + tensor(number, s, shift)

            step = (at(s, shift) - middle[s]) * (1.0 if shift > 0 else -1.0)
            other_x = at(s + 1, shift) - at(s - 1, shift)
            return (
                0.125 * mean(XY) * (grad_x + other_x)
                + 0.5 * mean(YY) * step
                + 0.125 * mean(YZ) * (grads_z[s] + grad_z(at(s, shift)))
            )

        upper = jnp.where(jnp.logical_and(y_row == by - 1, last_y), 0.0, face_y(1))
        lower = jnp.where(jnp.logical_and(y_row == 0, first_y), 0.0, face_y(-1))

        def pair(values):
            return values + next_z(values)

        face_z = (
            0.125 * pair(tensor(XZ, s)) * pair(grad_x)
            + 0.125 * pair(tensor(YZ, s)) * pair(grads_y[s])
            + 0.5 * pair(tensor(ZZ, s)) * (next_z(middle[s]) - middle[s])
        )
        face_z = jnp.where(z_lane == nz - 1, 0.0, face_z)
        divergent = (
            (faces[i + 1] - faces[i]) + (upper - lower) + (face_z - pltpu.roll(face_z, 1, 1))
        )
        voltage = middle[s]
        resting = rest_in[i]
        current = 8.0 * voltage * (voltage - 0.15) * (voltage - 1.0) + voltage * resting
        current = current + 10.0 * jnp.maximum(stretches[i] - 1.0, 0.0) * (voltage - 0.6)
        next_potential[i] = voltage + 0.1 * (divergent - current)
        next_recovery[i] = resting + 0.05 * (-resting - 8.0 * voltage * (voltage - 1.15))

    everything(lambda copy: copy.wait_send())


def solution(mesh):
    across, down = mesh.shape["gx"], mesh.shape["gy"]

    def local(potential, recovery, angles, deform, slots):
        bx, by, nz = potential.shape
        ex, ey, ez = slots.shape
        parts, count = deform.shape
        assert ex == 1 and bx == RATIO and by % 8 == 0 and count % LANES == 0
        sizes = (bx, by, nz, ex, ey, ez, parts, count)
        f32 = jnp.float32
        shape = jax.ShapeDtypeStruct(potential.shape, f32)
        copies = 3 * down + 27
        return pl.pallas_call(
            functools.partial(kernel, across, down, sizes),
            out_shape=(shape, shape),
            in_specs=[pl.BlockSpec(memory_space=pl.ANY)] * 5,
            out_specs=(pl.BlockSpec(memory_space=pltpu.VMEM),) * 2,
            scratch_shapes=[
                pltpu.VMEM((bx + 2, by + 16, nz), f32),
                pltpu.VMEM(recovery.shape, f32),
                pltpu.VMEM(angles.shape, f32),
                pltpu.VMEM((2, 2, by, nz), f32),
                pltpu.VMEM((2, 2, bx, 1, nz), f32),
                pltpu.VMEM((3, down, parts, count), f32),
                pltpu.VMEM((3, 3, ex, ey, ez), jnp.int32),
                pltpu.VMEM((3, bx + 2, by, nz), f32),
                pltpu.VMEM((6, bx + 2, by + 16, nz), f32),
                pltpu.VMEM((bx, by, nz), f32),
                pltpu.SemaphoreType.DMA((copies,)),
                pltpu.SemaphoreType.DMA((3 * down,)),
                pltpu.SemaphoreType.DMA((27,)),
                pltpu.SemaphoreType.DMA((5,)),
            ],
            compiler_params=pltpu.CompilerParams(collective_id=0, has_side_effects=True),
        )(potential, recovery, angles, deform, slots)

    return jax.shard_map(
        local,
        mesh=mesh,
        in_specs=(
            P("gx", "gy", None),
            P("gx", "gy", None),
            P(None, "gx", "gy", None),
            P(None, ("gx", "gy")),
            P("gx", "gy", None),
        ),
        out_specs=(P("gx", "gy", None), P("gx", "gy", None)),
        check_vma=False,
    )
```

time: 101 us -> 14.8 us (0.15)
  starting transfers between devices: 39.8 us -> 0 us
  local copies, waits for them, and re-layouts: 32.6 us -> 2.14 us
  other arithmetic: 17.9 us -> 0 us
  Pallas kernels: 0 us -> 11.9 us
  waiting for transfers between devices: 8.2 us -> 0 us
    ppermute x12 -> x0, starting transfers between devices: 30.5 us -> none  [the longest x6 22.7 us: padded_2(): lax.ppermute(lax.slice_in_dim(block, block.shape[dim] - width, None, axis...]
    slice x25 -> x0, local copies, waits for them, and re-layouts: 12.2 us -> none  [the longest x10 9.17 us: tensors(): entries = [field[number] for number in range(9)]]
    pallas_call x0 -> x1, Pallas kernels: none -> 11.9 us  [local(): pl.pallas_call(functools.partial(kernel, across, down, sizes), out_shape=...]
    all_to_all x2 -> x0, starting transfers between devices: 9.38 us -> none  [the longest x1 5.19 us: local(): lax.all_to_all(wanted, 'gy', split_axis=0, concat_axis=0, tiled=True)]
    squeeze x14 -> x0, local copies, waits for them, and re-layouts: 5.53 us -> none  [the longest x13 5.44 us: tensors(): entries = [field[number] for number in range(9)]]
    unnamed x41 -> x4, local copies, waits for them, and re-layouts: 7.11 us -> 2.14 us
    all_to_all x2 -> x0, waiting for transfers between devices: 4.19 us -> none  [the longest x1 4.19 us: local(): lax.all_to_all(picked, 'gy', split_axis=1, concat_axis=1, tiled=True)]
    ppermute x12 -> x0, waiting for transfers between devices: 4 us -> none  [the longest x6 3.99 us: padded_2(): lax.ppermute(lax.slice_in_dim(block, 0, width, axis=dim), axis, backward)]
  transfers between devices with their start and end apart: 14 -> 0, of which waited for: 2 -> 0; matrix products, arithmetic and copies ran while one was open for 33% -> 0% of each run, Pallas kernels for 0% -> 0%
where the time goes in v1:
time: 14.8 us; the launch traced here: 14.6 us
  Pallas kernels  11.9 us (80%)
  local copies, waits for them, and re-layouts  2.14 us (14%)
  between operations  0.65 us (4%)
    pallas_call x1, Pallas kernels, local(): pl.pallas_call(functools.partial(kernel, across, down, sizes), out_shape=...  11.9 us
    unnamed x4, local copies, waits for them, and re-layouts  2.14 us

profile of v1, /device:TPU:0, one launch (start us, length us, event | category | flops | bytes accessed | tf_op | source)
XLA Modules:
  0.0 14.6 jit_solution(7410671865252144264)
XLA Ops:
  0.6 11.9 %shard_map.68 = (f32[4,16,256]{2,1,0:T(8,128)}, f32[4,16,256]{2,1,0:T(8,128)}) custom-call(f32[4,16,256]{2,1,0:T(8,128)} %potential.1, f32[4,16,256]{2,1,0:T(8,128)} %recovery.1, f32[2,4,16,256]{3,2,1,0:T(8,128)} %angles.1, f32[9,256]{1,0:T(8,128)} %deform.1, s32[1,4,64]{2,1,0:T(4,128)} %slots.1), custom_call_target="tpu_custom_call" | custom-call | tf_op jit(solution)/shard_map/pallas_call | solution.py:434
  12.5 0.0 copy-start
  12.5 1.5 %copy.9 = f32[4,16,256]{2,1,0:T(8,128)} copy(f32[4,16,256]{2,1,0:T(8,128)} %get-tuple-element.4) | data formatting | bytes 131072
  14.0 0.0 copy-done
  14.0 0.6 %copy.10 = f32[4,16,256]{2,1,0:T(8,128)} copy(f32[4,16,256]{2,1,0:T(8,128)S(1)} %copy-done) | data formatting | bytes 131072
Async XLA Ops:
  12.5 1.5 %copy-start = (f32[4,16,256]{2,1,0:T(8,128)S(1)}, f32[4,16,256]{2,1,0:T(8,128)}, u32[]{:S(2)}) copy-start(f32[4,16,256]{2,1,0:T(8,128)} %get-tuple-element.5) | copy-start | bytes 196612

commit v2 on v1

--- a/solution.py
+++ b/solution.py
@@ -10,6 +10,7 @@
 MESH = pl.DeviceIdType.MESH
 RATIO = 4
 LANES = 128
+VMEM_LIMIT = 16 * 1024 * 1024
 TOP = 8
 
 SIDES = tuple((dx, dy) for dx in (-1, 0, 1) for dy in (-1, 0, 1) if (dx, dy) != (0, 0))
@@ -103,7 +104,7 @@
     return jnp.sqrt(parts[0] * parts[0] + parts[1] * parts[1] + parts[2] * parts[2])
 
 
-def kernel(
+def exchange(
     across,
     down,
     sizes,
@@ -112,24 +113,20 @@
     angles,
     deform,
     slots,
-    next_potential,
-    next_recovery,
-    volts,
+    cells,
     rest_in,
-    own_angles,
-    x_angles,
-    y_angles,
     held,
     near_slots,
     fibers,
-    conducts,
-    stretches,
+    spread_y,
+    spread_z,
     send_sem,
     deform_sem,
     near_sem,
     local_sem,
 ):
     bx, by, nz, ex, ey, ez, parts, count = sizes
+    blocks = count // LANES
     gx, gy = lax.axis_index("gx"), lax.axis_index("gy")
     first_x, last_x = gx == 0, gx == across - 1
     first_y, last_y = gy == 0, gy == down - 1
@@ -153,29 +150,38 @@
             pl.semaphore_signal(barrier, inc=1, device_id=(gx + dx, target), device_id_type=MESH)
 
     pl.when(exists(-1, 0))(lambda: greet(-1))
+    pl.when(exists(1, 0))(lambda: greet(1))
     greet(0)
-    pl.when(exists(1, 0))(lambda: greet(1))
-
-    own = [
-        pltpu.make_async_copy(
-            potential, volts.at[pl.ds(1, bx), pl.ds(TOP, by), :], local_sem.at[0]
-        ),
-        pltpu.make_async_copy(recovery, rest_in, local_sem.at[1]),
-        pltpu.make_async_copy(angles, own_angles, local_sem.at[2]),
-        pltpu.make_async_copy(deform, held.at[1, gy], local_sem.at[3]),
-        pltpu.make_async_copy(slots, near_slots.at[1, 1], local_sem.at[4]),
-    ]
-    for copy in (own[2], own[4], own[3], own[0], own[1]):
+
+    packed = held.at[1, gy]
+    local = []
+
+    def fetch(source, target):
+        copy = pltpu.make_async_copy(source, target, local_sem.at[len(local)])
         copy.start()
+        local.append(copy)
+
+    for b in range(blocks):
+        columns = pl.ds(b * LANES, LANES)
+        fetch(deform.at[pl.ds(0, 8), columns], packed.at[pl.ds(8 * b, 8)])
+        fetch(deform.at[pl.ds(8, 1), columns], packed.at[pl.ds(8 * blocks + b, 1)])
+    fetch(slots, near_slots.at[1, 1])
+    inside = pl.ds(TOP, by)
+    fetch(potential, cells.at[0, pl.ds(1, bx), inside])
+    fetch(angles, cells.at[pl.ds(1, 2), pl.ds(1, bx), inside])
+    fetch(recovery, rest_in)
+    for copy in local:
+        copy.wait()
 
     rows_here = 1 + jnp.where(first_x, 0, 1) + jnp.where(last_x, 0, 1)
     pl.semaphore_wait(barrier, rows_here * down - 1)
 
     def deform_copy(dx, step, target):
         index = (1 - dx) * down + step
+        rows = pl.ds(0, 9 * blocks)
         return pltpu.make_async_remote_copy(
-            src_ref=deform,
-            dst_ref=held.at[1 - dx, gy],
+            src_ref=held.at[1, gy, rows],
+            dst_ref=held.at[1 - dx, gy, rows],
             send_sem=send_sem.at[index],
             recv_sem=deform_sem.at[index],
             device_id=(gx + dx, target),
@@ -184,25 +190,22 @@
 
     def near_copies(dx, dy):
         place = (1 - dx) * 3 + (1 - dy)
-        base = 3 * down + 3 * place
-        x_source = pl.ds(0, bx) if dx == 0 else pl.ds(0 if dx < 0 else bx - 1, 1)
+        base = 3 * down + 2 * place
+        x_source = pl.ds(1, bx) if dx == 0 else pl.ds(1 if dx < 0 else bx, 1)
         x_target = pl.ds(1, bx) if dx == 0 else pl.ds(bx + 1 if dx < 0 else 0, 1)
-        y_source = pl.ds(0, by) if dy == 0 else pl.ds(0 if dy < 0 else by - 1, 1)
-        y_target = pl.ds(TOP, by) if dy == 0 else pl.ds(TOP + by if dy < 0 else TOP - 1, 1)
+        y_source = inside if dy == 0 else pl.ds(TOP if dy < 0 else TOP + by - 1, 1)
+        y_target = inside if dy == 0 else pl.ds(TOP + by if dy < 0 else TOP - 1, 1)
+        fields = pl.ds(0, 1 if dx and dy else 3)
         pairs = [
-            (slots, near_slots.at[1 - dx, 1 - dy]),
-            (potential.at[x_source, y_source, :], volts.at[x_target, y_target, :]),
+            (near_slots.at[1, 1], near_slots.at[1 - dx, 1 - dy]),
+            (cells.at[fields, x_source, y_source], cells.at[fields, x_target, y_target]),
         ]
-        if dy == 0:
-            pairs.append((angles.at[:, x_source], x_angles.at[:, pl.ds(1 if dx < 0 else 0, 1)]))
-        elif dx == 0:
-            pairs.append((angles.at[:, :, y_source], y_angles.at[1 if dy < 0 else 0]))
         return [
             pltpu.make_async_remote_copy(
                 src_ref=source,
                 dst_ref=target,
                 send_sem=send_sem.at[base + number],
-                recv_sem=near_sem.at[3 * place + number],
+                recv_sem=near_sem.at[2 * place + number],
                 device_id=(gx + dx, gy + dy),
                 device_id_type=MESH,
             )
@@ -221,7 +224,7 @@
         def side(dx, dy):
             pl.when(exists(way * dx, way * dy))(lambda: over_near(dx, dy, act))
 
-        for dx in (-1, 0, 1):
+        for dx in (-1, 1, 0):
             if dx:
                 pl.when(exists(way * dx, 0))(lambda dx=dx: over_row(dx, act))
             else:
@@ -237,50 +240,91 @@
     lane = lax.broadcasted_iota(jnp.int32, (tall, width), 1)
     cell = jnp.where(row < by, row, jnp.where(row < by + bx, -1, by))
     spot = (cell.astype(jnp.float32) + 0.5) * (1.0 / RATIO) - 0.5
-    weight_y = jnp.maximum(1.0 - jnp.abs(spot - ((lane // ez) - 1).astype(jnp.float32)), 0.0)
+    spread_y[...] = jnp.maximum(
+        1.0 - jnp.abs(spot - ((lane // ez) - 1).astype(jnp.float32)), 0.0
+    )
     row = lax.broadcasted_iota(jnp.int32, (width, nz), 0)
     lane = lax.broadcasted_iota(jnp.int32, (width, nz), 1)
     spot = jnp.clip((lane.astype(jnp.float32) + 0.5) * (1.0 / RATIO) - 0.5, 0.0, ez - 1.0)
-    weight_z = jnp.maximum(1.0 - jnp.abs(spot - lax.rem(row, ez).astype(jnp.float32)), 0.0)
-    weight_z = weight_z.astype(jnp.bfloat16)
-
-    own[2].wait()
+    weight = jnp.maximum(1.0 - jnp.abs(spot - lax.rem(row, ez).astype(jnp.float32)), 0.0)
+    spread_z[...] = weight.astype(jnp.bfloat16)
+
     for s in range(bx):
-        for number, part in enumerate(fiber_of(own_angles[0, s], own_angles[1, s])):
-            fibers[number, s + 1] = part
-
-    for number in (4, 3, 0, 1):
-        own[number].wait()
+        own = [cells[number, s + 1, TOP : TOP + by] for number in (1, 2)]
+        for number, part in enumerate(fiber_of(*own)):
+            fibers[number, s] = part
 
     everything(lambda copy: copy.wait_recv(), -1)
+    everything(lambda copy: copy.wait_send())
+
+
+def compute(
+    across,
+    down,
+    sizes,
+    cells,
+    rest_in,
+    held,
+    near_slots,
+    fibers,
+    spread_y,
+    spread_z,
+    next_potential,
+    next_recovery,
+    volts,
+    conducts,
+    out_potential,
+    out_recovery,
+    out_sem,
+):
+    bx, by, nz, ex, ey, ez, parts, count = sizes
+    blocks = count // LANES
+    gx, gy = lax.axis_index("gx"), lax.axis_index("gy")
+    first_x, last_x = gx == 0, gx == across - 1
+    first_y, last_y = gy == 0, gy == down - 1
+    width = (ey + 2) * ez
+    tall = by + 8
+
+    for i in range(bx):
+        voltage = cells[0, i + 1, TOP : TOP + by]
+        resting = rest_in[i]
+        out_recovery[i] = resting + 0.05 * (-resting - 8.0 * voltage * (voltage - 1.15))
+    leaving = [pltpu.make_async_copy(out_recovery, next_recovery, out_sem.at[bx])]
+    leaving[0].start()
 
     gathered = []
     digits = lax.broadcasted_iota(jnp.int32, (LANES, width), 0)
-    blocks = count // LANES
+    pages = down * blocks
     for q in range(3):
         low = jnp.where(first_y, near_slots[q, 1, 0, 0:1], near_slots[q, 0, 0, ey - 1 : ey])
         high = jnp.where(last_y, near_slots[q, 1, 0, ey - 1 : ey], near_slots[q, 2, 0, 0:1])
         pieces = [low] + [near_slots[q, 1, 0, c : c + 1] for c in range(ey)] + [high]
         index = jnp.concatenate(pieces, axis=1) - (gx + q - 1) * (down * count)
         chosen = (digits == (index & (LANES - 1))).astype(jnp.float32).astype(jnp.bfloat16)
-        table = []
-        for h in range(down):
-            block = held[q, h]
-            block = jnp.concatenate([block, jnp.zeros((16 - parts, count), jnp.float32)], axis=0)
-            table += [block[:, b * LANES : (b + 1) * LANES] for b in range(blocks)]
+        table = [held[q, h, 0 : 8 * blocks] for h in range(down)]
+        table += [held[q, h, 8 * blocks : 9 * blocks] for h in range(down)]
         found = dot_two(jnp.concatenate(table, axis=0), chosen)
         page = index >> (LANES.bit_length() - 1)
-        total = jnp.zeros((16, width), jnp.float32)
-        for h in range(down * blocks):
-            total = jnp.where(page == h, found[16 * h : 16 * h + 16], total)
-        gathered.append(total)
-    gathered[0] = jnp.where(first_x, gathered[1], gathered[0])
-    gathered[2] = jnp.where(last_x, gathered[1], gathered[2])
+        total = jnp.zeros((8, width), jnp.float32)
+        for h in range(pages):
+            total = jnp.where(page == h, found[8 * h : 8 * h + 8], total)
+        last = found[8 * pages : 9 * pages]
+        kept = lax.broadcasted_iota(jnp.int32, (pages, width), 0) == page
+        last = jnp.sum(jnp.where(kept, last, 0.0), axis=0, keepdims=True)
+        gathered.append([total, last])
+    for part in range(2):
+        gathered[0][part] = jnp.where(first_x, gathered[1][part], gathered[0][part])
+        gathered[2][part] = jnp.where(last_x, gathered[1][part], gathered[2][part])
 
     refined = []
+    weight_y = spread_y[...]
+    weight_z = spread_z[...]
     for q in range(3):
-        spread = [weight_y * gathered[q][k : k + 1] for k in range(parts)]
+        total, last = gathered[q]
+        spread = [weight_y * total[k : k + 1] for k in range(8)] + [weight_y * last]
         refined.append(dot_two(jnp.concatenate(spread, axis=0), weight_z))
+
+    volts[...] = cells[0, :, 0:by + 16]
 
     @pl.when(first_y)
     def _():
@@ -298,13 +342,11 @@
     def _():
         volts[bx + 1] = volts[bx]
 
-    for side, s in ((0, 0), (1, bx + 1)):
-        for number, part in enumerate(fiber_of(x_angles[0, side], x_angles[1, side])):
-            fibers[number, s] = part
-    rim = [
-        jnp.concatenate([y_angles[side, c, s] for side in range(2) for s in range(bx)], axis=0)
-        for c in range(2)
-    ]
+    def rim_of(number):
+        rows = [cells[number, s + 1, row : row + 1] for row in (TOP - 1, TOP + by) for s in range(bx)]
+        return jnp.concatenate(rows, axis=0)
+
+    rim = [rim_of(1), rim_of(2)]
     rim_fiber = fiber_of(rim[0], rim[1])
 
     def hat(s):
@@ -320,11 +362,14 @@
                 at = tall * k + 8 * half
                 terms = [w * refined[q][at : at + 8] for q, w in enumerate(weights) if w]
                 entries.append(functools.reduce(jnp.add, terms))
-            fiber = [fibers[number, s, rows] for number in range(3)]
+            if 1 <= s <= bx:
+                fiber = [fibers[number, s - 1, rows] for number in range(3)]
+            else:
+                fiber = fiber_of(*(cells[number, s, TOP + 8 * half : TOP + 8 * half + 8] for number in (1, 2)))
             for number, value in enumerate(tensor_of(entries, fiber)):
                 conducts[number, s, TOP + 8 * half : TOP + 8 * half + 8] = value
             if 1 <= s <= bx:
-                stretches[s - 1, rows] = stretch_of(entries, fiber)
+                out_potential[s - 1, rows] = stretch_of(entries, fiber)
     rim_row = lax.rem(lax.broadcasted_iota(jnp.int32, (2 * bx, nz), 0), bx).astype(jnp.float32)
     spot = (rim_row + 0.5) * (1.0 / RATIO) - 0.5
     rim_weights = [jnp.maximum(1.0 - jnp.abs(spot - (q - 1.0)), 0.0) for q in range(3)]
@@ -412,11 +457,13 @@
         voltage = middle[s]
         resting = rest_in[i]
         current = 8.0 * voltage * (voltage - 0.15) * (voltage - 1.0) + voltage * resting
-        current = current + 10.0 * jnp.maximum(stretches[i] - 1.0, 0.0) * (voltage - 0.6)
-        next_potential[i] = voltage + 0.1 * (divergent - current)
-        next_recovery[i] = resting + 0.05 * (-resting - 8.0 * voltage * (voltage - 1.15))
-
-    everything(lambda copy: copy.wait_send())
+        current = current + 10.0 * jnp.maximum(out_potential[i] - 1.0, 0.0) * (voltage - 0.6)
+        out_potential[i] = voltage + 0.1 * (divergent - current)
+        copy = pltpu.make_async_copy(out_potential.at[i], next_potential.at[i], out_sem.at[i])
+        copy.start()
+        leaving.append(copy)
+    for copy in leaving:
+        copy.wait()
 
 
 def solution(mesh):
@@ -426,34 +473,52 @@
         bx, by, nz = potential.shape
         ex, ey, ez = slots.shape
         parts, count = deform.shape
-        assert ex == 1 and bx == RATIO and by % 8 == 0 and count % LANES == 0
+        assert ex == 1 and bx == RATIO and by % 8 == 0 and count % LANES == 0 and parts == 9
         sizes = (bx, by, nz, ex, ey, ez, parts, count)
+        blocks = count // LANES
+        width = (ey + 2) * ez
         f32 = jnp.float32
         shape = jax.ShapeDtypeStruct(potential.shape, f32)
-        copies = 3 * down + 27
+        anywhere = pl.BlockSpec(memory_space=pl.ANY)
+        in_vmem = pl.BlockSpec(memory_space=pltpu.VMEM)
+        passed = (
+            pltpu.VMEM((3, bx + 2, by + 16, nz), f32),
+            pltpu.VMEM(recovery.shape, f32),
+            pltpu.VMEM((3, down, 8 * blocks + 8, LANES), f32),
+            pltpu.VMEM((3, 3, ex, ey, ez), jnp.int32),
+            pltpu.VMEM((3, bx, by, nz), f32),
+            pltpu.VMEM((by + 8, width), f32),
+            pltpu.VMEM((width, nz), jnp.bfloat16),
+        )
+        arrived = pl.pallas_call(
+            functools.partial(exchange, across, down, sizes),
+            out_shape=passed,
+            in_specs=[pl.BlockSpec(memory_space=pltpu.MemorySpace.HBM)] * 5,
+            out_specs=(in_vmem,) * len(passed),
+            scratch_shapes=[
+                pltpu.SemaphoreType.DMA((3 * down + 18,)),
+                pltpu.SemaphoreType.DMA((3 * down,)),
+                pltpu.SemaphoreType.DMA((18,)),
+                pltpu.SemaphoreType.DMA((2 * blocks + 4,)),
+            ],
+            compiler_params=pltpu.CompilerParams(
+                collective_id=0, has_side_effects=True, vmem_limit_bytes=VMEM_LIMIT
+            ),
+        )(*(pltpu.with_memory_space_constraint(x, pltpu.MemorySpace.HBM) for x in (potential, recovery, angles, deform, slots)))
         return pl.pallas_call(
-            functools.partial(kernel, across, down, sizes),
+            functools.partial(compute, across, down, sizes),
             out_shape=(shape, shape),
-            in_specs=[pl.BlockSpec(memory_space=pl.ANY)] * 5,
-            out_specs=(pl.BlockSpec(memory_space=pltpu.VMEM),) * 2,
+            in_specs=[in_vmem] * len(passed),
+            out_specs=(anywhere,) * 2,
             scratch_shapes=[
                 pltpu.VMEM((bx + 2, by + 16, nz), f32),
-                pltpu.VMEM(recovery.shape, f32),
-                pltpu.VMEM(angles.shape, f32),
-                pltpu.VMEM((2, 2, by, nz), f32),
-                pltpu.VMEM((2, 2, bx, 1, nz), f32),
-                pltpu.VMEM((3, down, parts, count), f32),
-                pltpu.VMEM((3, 3, ex, ey, ez), jnp.int32),
-                pltpu.VMEM((3, bx + 2, by, nz), f32),
                 pltpu.VMEM((6, bx + 2, by + 16, nz), f32),
                 pltpu.VMEM((bx, by, nz), f32),
-                pltpu.SemaphoreType.DMA((copies,)),
-                pltpu.SemaphoreType.DMA((3 * down,)),
-                pltpu.SemaphoreType.DMA((27,)),
-                pltpu.SemaphoreType.DMA((5,)),
+                pltpu.VMEM((bx, by, nz), f32),
+                pltpu.SemaphoreType.DMA((bx + 1,)),
             ],
-            compiler_params=pltpu.CompilerParams(collective_id=0, has_side_effects=True),
-        )(potential, recovery, angles, deform, slots)
+            compiler_params=pltpu.CompilerParams(vmem_limit_bytes=VMEM_LIMIT),
+        )(*arrived)
 
     return jax.shard_map(
         local,

time: 14.8 us -> 11.4 us (0.77)
  the two profiles are of different devices: /device:TPU:0 before, /device:TPU:1 now
where the time goes in v2:
time: 11.4 us; the launch traced here: 11.3 us
  Pallas kernels  10.6 us (93%)
  between operations  0.64 us (6%)
    pallas_call x1, Pallas kernels, local(): pl.pallas_call(functools.partial(exchange, across, down, sizes), out_shap...  8.08 us
    pallas_call x1, Pallas kernels, local(): pl.pallas_call(functools.partial(compute, across, down, sizes), out_shape...  2.55 us

profile of v2, /device:TPU:1, one launch (start us, length us, event | category | flops | bytes accessed | tf_op | source)
XLA Modules:
  0.0 11.3 jit_solution(3959617594519661363)
XLA Ops:
  0.6 8.1 %shard_map.68 = (f32[3,6,32,256]{3,2,1,0:T(8,128)S(1)}, f32[4,16,256]{2,1,0:T(8,128)S(1)}, f32[3,4,24,128]{3,2,1,0:T(8,128)S(1)}, s32[3,3,1,4,64]{4,3,2,1,0:T(4,...) custom-call(f32[4,16,256]{2,1,0:T(8,128)} %potential.1, ...), custom_call_target="tpu_custom_call" | custom-call | tf_op jit(solution)/shard_map/pallas_call | solution.py:493
  8.7 2.5 %shard_map.69 = (f32[4,16,256]{2,1,0:T(8,128)}, f32[4,16,256]{2,1,0:T(8,128)}) custom-call(f32[3,6,32,256]{3,2,1,0:T(8,128)S(1)} %get-tuple-element.9.cells, f32[4,16,256]{2,1,0:T(8,128)S(1)} %get-tuple-element.10.rest_in, f32[3,4,24,128]{3,2,1,0:T(8,128)S(1)} %get-tuple-element.11.held, s32[3,3,1,4,64]{4,3,2,1,0:T(4,128)S(1)} %get-tuple-element.12.near_slots, ...), custom_call_target="tpu_custom_call" | custom-call | tf_op jit(solution)/shard_map/pallas_call | solution.py:508

commit v3 on v2

--- a/solution.py
+++ b/solution.py
@@ -104,6 +104,30 @@
     return jnp.sqrt(parts[0] * parts[0] + parts[1] * parts[1] + parts[2] * parts[2])
 
 
+def gather_refined(held, q, chosen, page, weight_z, sizes, down):
+    bx, by, nz, ex, ey, ez, parts, count = sizes
+    blocks = count // LANES
+    pages = down * blocks
+    width = (ey + 2) * ez
+    table = [held[q, h, 0 : 8 * blocks] for h in range(down)]
+    table += [held[q, h, 8 * blocks : 9 * blocks] for h in range(down)]
+    found = dot_two(jnp.concatenate(table, axis=0), chosen)
+    total = jnp.zeros((8, width), jnp.float32)
+    for h in range(pages):
+        total = jnp.where(page == h, found[8 * h : 8 * h + 8], total)
+    kept = lax.broadcasted_iota(jnp.int32, (pages, width), 0) == page
+    last = jnp.sum(jnp.where(kept, found[8 * pages : 9 * pages], 0.0), axis=0, keepdims=True)
+    row = lax.broadcasted_iota(jnp.int32, (8, width), 0)
+    here = row == lax.broadcasted_iota(jnp.int32, (8, width), 1) // ez
+    spread = [jnp.where(here, total[k : k + 1], 0.0) for k in range(8)]
+    spread.append(jnp.where(here, last, 0.0))
+    return dot_two(jnp.concatenate(spread, axis=0), weight_z)
+
+
+def hat(distance):
+    return jnp.maximum(1.0 - jnp.abs(distance), 0.0)
+
+
 def exchange(
     across,
     down,
@@ -113,13 +137,20 @@
     angles,
     deform,
     slots,
+    volts,
+    base,
+    new_recovery,
+    held,
+    chosen,
+    pages,
+    fibers,
+    rim_fibers,
+    spread_xy,
+    spread_z,
+    own_refined,
     cells,
     rest_in,
-    held,
     near_slots,
-    fibers,
-    spread_y,
-    spread_z,
     send_sem,
     deform_sem,
     near_sem,
@@ -170,6 +201,23 @@
     fetch(potential, cells.at[0, pl.ds(1, bx), inside])
     fetch(angles, cells.at[pl.ds(1, 2), pl.ds(1, bx), inside])
     fetch(recovery, rest_in)
+    width = (ey + 2) * ez
+    main = (bx + 2) * by
+    row = lax.broadcasted_iota(jnp.int32, spread_xy.shape, 0)
+    lane = lax.broadcasted_iota(jnp.int32, spread_xy.shape, 1)
+    inner = row < main
+    x_cell = jnp.where(inner, row // by - 1, lax.rem(row - main, bx))
+    y_cell = jnp.where(inner, lax.rem(row, by), jnp.where(row < main + bx, -1, by))
+    x_spot = (x_cell.astype(jnp.float32) + 0.5) * (1.0 / RATIO) + 0.5
+    y_spot = (y_cell.astype(jnp.float32) + 0.5) * (1.0 / RATIO) + 0.5
+    x_weight = hat(x_spot - (lax.rem(lane, 24) // 8).astype(jnp.float32))
+    y_weight = hat(y_spot - lax.rem(lane, 8).astype(jnp.float32))
+    spread_xy[...] = (x_weight * y_weight).astype(jnp.bfloat16)
+    row = lax.broadcasted_iota(jnp.int32, (width, nz), 0)
+    lane = lax.broadcasted_iota(jnp.int32, (width, nz), 1)
+    spot = jnp.clip((lane.astype(jnp.float32) + 0.5) * (1.0 / RATIO) - 0.5, 0.0, ez - 1.0)
+    spread_z[...] = hat(spot - lax.rem(row, ez).astype(jnp.float32)).astype(jnp.bfloat16)
+
     for copy in local:
         copy.wait()
 
@@ -220,61 +268,99 @@
         for copy in near_copies(dx, dy):
             act(copy)
 
-    def everything(act, way=1):
-        def side(dx, dy):
-            pl.when(exists(way * dx, way * dy))(lambda: over_near(dx, dy, act))
-
-        for dx in (-1, 1, 0):
-            if dx:
-                pl.when(exists(way * dx, 0))(lambda dx=dx: over_row(dx, act))
-            else:
-                over_row(0, act)
+    def far_rows(act, way=1):
+        for dx in (-1, 1):
+            pl.when(exists(way * dx, 0))(lambda dx=dx: over_row(dx, act))
+
+    def all_near(act, way=1):
         for dx, dy in SIDES:
-            side(dx, dy)
-
-    everything(lambda copy: copy.start())
-
-    width = (ey + 2) * ez
-    tall = by + 8
-    row = lax.broadcasted_iota(jnp.int32, (tall, width), 0)
-    lane = lax.broadcasted_iota(jnp.int32, (tall, width), 1)
-    cell = jnp.where(row < by, row, jnp.where(row < by + bx, -1, by))
-    spot = (cell.astype(jnp.float32) + 0.5) * (1.0 / RATIO) - 0.5
-    spread_y[...] = jnp.maximum(
-        1.0 - jnp.abs(spot - ((lane // ez) - 1).astype(jnp.float32)), 0.0
-    )
-    row = lax.broadcasted_iota(jnp.int32, (width, nz), 0)
-    lane = lax.broadcasted_iota(jnp.int32, (width, nz), 1)
-    spot = jnp.clip((lane.astype(jnp.float32) + 0.5) * (1.0 / RATIO) - 0.5, 0.0, ez - 1.0)
-    weight = jnp.maximum(1.0 - jnp.abs(spot - lax.rem(row, ez).astype(jnp.float32)), 0.0)
-    spread_z[...] = weight.astype(jnp.bfloat16)
-
-    for s in range(bx):
-        own = [cells[number, s + 1, TOP : TOP + by] for number in (1, 2)]
-        for number, part in enumerate(fiber_of(*own)):
+            pl.when(exists(way * dx, way * dy))(lambda dx=dx, dy=dy: over_near(dx, dy, act))
+
+    all_near(lambda copy: copy.start())
+    far_rows(lambda copy: copy.start())
+    over_row(0, lambda copy: copy.start())
+
+    def slice_fiber(s):
+        angle = [cells[number, s, TOP : TOP + by] for number in (1, 2)]
+        for number, part in enumerate(fiber_of(*angle)):
             fibers[number, s] = part
 
-    everything(lambda copy: copy.wait_recv(), -1)
-    everything(lambda copy: copy.wait_send())
+    for s in range(1, bx + 1):
+        slice_fiber(s)
+        voltage = cells[0, s, TOP : TOP + by]
+        resting = rest_in[s - 1]
+        current = 8.0 * voltage * (voltage - 0.15) * (voltage - 1.0) + voltage * resting
+        base[s - 1] = voltage - 0.1 * current
+        new_recovery[s - 1] = resting + 0.05 * (-resting - 8.0 * voltage * (voltage - 1.15))
+
+    all_near(lambda copy: copy.wait_recv(), -1)
+
+    volts[...] = cells[0]
+
+    @pl.when(first_y)
+    def _():
+        volts[:, TOP - 1 : TOP] = volts[:, TOP : TOP + 1]
+
+    @pl.when(last_y)
+    def _():
+        volts[:, TOP + by : TOP + by + 1] = volts[:, TOP + by - 1 : TOP + by]
+
+    @pl.when(first_x)
+    def _():
+        volts[0] = volts[1]
+
+    @pl.when(last_x)
+    def _():
+        volts[bx + 1] = volts[bx]
+
+    slice_fiber(0)
+    slice_fiber(bx + 1)
+
+    def rim_of(number):
+        rows = [
+            cells[number, s + 1, row : row + 1] for row in (TOP - 1, TOP + by) for s in range(bx)
+        ]
+        return jnp.concatenate(rows, axis=0)
+
+    for number, part in enumerate(fiber_of(rim_of(1), rim_of(2))):
+        rim_fibers[number] = part
+
+    digits = lax.broadcasted_iota(jnp.int32, (LANES, width), 0)
+    for q in range(3):
+        low = jnp.where(first_y, near_slots[q, 1, 0, 0:1], near_slots[q, 0, 0, ey - 1 : ey])
+        high = jnp.where(last_y, near_slots[q, 1, 0, ey - 1 : ey], near_slots[q, 2, 0, 0:1])
+        pieces = [low] + [near_slots[q, 1, 0, c : c + 1] for c in range(ey)] + [high]
+        index = jnp.concatenate(pieces, axis=1) - (gx + q - 1) * (down * count)
+        hit = digits == (index & (LANES - 1))
+        chosen[q] = hit.astype(jnp.float32).astype(jnp.bfloat16)
+        pages[q] = index >> (LANES.bit_length() - 1)
+
+    over_row(0, lambda copy: copy.wait_recv())
+    far_rows(lambda copy: copy.wait_recv(), -1)
+    far_rows(lambda copy: copy.wait_send())
+    over_row(0, lambda copy: copy.wait_send())
+    all_near(lambda copy: copy.wait_send())
 
 
 def compute(
     across,
     down,
     sizes,
-    cells,
-    rest_in,
+    volts,
+    base,
+    new_recovery,
     held,
-    near_slots,
+    chosen,
+    pages,
     fibers,
-    spread_y,
+    rim_fibers,
+    spread_xy,
     spread_z,
+    own_refined,
     next_potential,
     next_recovery,
-    volts,
     conducts,
     out_potential,
-    out_recovery,
     out_sem,
 ):
     bx, by, nz, ex, ey, ez, parts, count = sizes
@@ -282,105 +368,38 @@
     gx, gy = lax.axis_index("gx"), lax.axis_index("gy")
     first_x, last_x = gx == 0, gx == across - 1
     first_y, last_y = gy == 0, gy == down - 1
-    width = (ey + 2) * ez
-    tall = by + 8
-
-    for i in range(bx):
-        voltage = cells[0, i + 1, TOP : TOP + by]
-        resting = rest_in[i]
-        out_recovery[i] = resting + 0.05 * (-resting - 8.0 * voltage * (voltage - 1.15))
-    leaving = [pltpu.make_async_copy(out_recovery, next_recovery, out_sem.at[bx])]
+    leaving = [pltpu.make_async_copy(new_recovery, next_recovery, out_sem.at[bx])]
     leaving[0].start()
 
-    gathered = []
-    digits = lax.broadcasted_iota(jnp.int32, (LANES, width), 0)
-    pages = down * blocks
-    for q in range(3):
-        low = jnp.where(first_y, near_slots[q, 1, 0, 0:1], near_slots[q, 0, 0, ey - 1 : ey])
-        high = jnp.where(last_y, near_slots[q, 1, 0, ey - 1 : ey], near_slots[q, 2, 0, 0:1])
-        pieces = [low] + [near_slots[q, 1, 0, c : c + 1] for c in range(ey)] + [high]
-        index = jnp.concatenate(pieces, axis=1) - (gx + q - 1) * (down * count)
-        chosen = (digits == (index & (LANES - 1))).astype(jnp.float32).astype(jnp.bfloat16)
-        table = [held[q, h, 0 : 8 * blocks] for h in range(down)]
-        table += [held[q, h, 8 * blocks : 9 * blocks] for h in range(down)]
-        found = dot_two(jnp.concatenate(table, axis=0), chosen)
-        page = index >> (LANES.bit_length() - 1)
-        total = jnp.zeros((8, width), jnp.float32)
-        for h in range(pages):
-            total = jnp.where(page == h, found[8 * h : 8 * h + 8], total)
-        last = found[8 * pages : 9 * pages]
-        kept = lax.broadcasted_iota(jnp.int32, (pages, width), 0) == page
-        last = jnp.sum(jnp.where(kept, last, 0.0), axis=0, keepdims=True)
-        gathered.append([total, last])
-    for part in range(2):
-        gathered[0][part] = jnp.where(first_x, gathered[1][part], gathered[0][part])
-        gathered[2][part] = jnp.where(last_x, gathered[1][part], gathered[2][part])
-
+    weight_z = spread_z[...]
+    own = gather_refined(held, 1, chosen[1], pages[1], weight_z, sizes, down)
+    low, high = (
+        gather_refined(held, q, chosen[q], pages[q], weight_z, sizes, down) for q in (0, 2)
+    )
+    low = jnp.where(first_x, own, low)
+    high = jnp.where(last_x, own, high)
+    weight_xy = spread_xy[...]
     refined = []
-    weight_y = spread_y[...]
-    weight_z = spread_z[...]
-    for q in range(3):
-        total, last = gathered[q]
-        spread = [weight_y * total[k : k + 1] for k in range(8)] + [weight_y * last]
-        refined.append(dot_two(jnp.concatenate(spread, axis=0), weight_z))
-
-    volts[...] = cells[0, :, 0:by + 16]
-
-    @pl.when(first_y)
-    def _():
-        volts[:, TOP - 1 : TOP] = volts[:, TOP : TOP + 1]
-
-    @pl.when(last_y)
-    def _():
-        volts[:, TOP + by : TOP + by + 1] = volts[:, TOP + by - 1 : TOP + by]
-
-    @pl.when(first_x)
-    def _():
-        volts[0] = volts[1]
-
-    @pl.when(last_x)
-    def _():
-        volts[bx + 1] = volts[bx]
-
-    def rim_of(number):
-        rows = [cells[number, s + 1, row : row + 1] for row in (TOP - 1, TOP + by) for s in range(bx)]
-        return jnp.concatenate(rows, axis=0)
-
-    rim = [rim_of(1), rim_of(2)]
-    rim_fiber = fiber_of(rim[0], rim[1])
-
-    def hat(s):
-        spot = (s + 0.5) / RATIO - 0.5
-        return [max(0.0, 1.0 - abs(spot - (q - 1))) for q in range(3)]
+    for k in range(parts):
+        rows = slice(8 * k, 8 * k + 8)
+        stack = jnp.concatenate([low[rows], own[rows], high[rows]], axis=0)
+        front = stack.astype(jnp.bfloat16).astype(jnp.float32)
+        stack = jnp.concatenate([front, stack - front], axis=0).astype(jnp.bfloat16)
+        refined.append(jnp.dot(weight_xy, stack, preferred_element_type=jnp.float32))
 
     for s in range(bx + 2):
-        weights = hat(s - 1)
         for half in range(by // 8):
             rows = slice(8 * half, 8 * half + 8)
-            entries = []
-            for k in range(parts):
-                at = tall * k + 8 * half
-                terms = [w * refined[q][at : at + 8] for q, w in enumerate(weights) if w]
-                entries.append(functools.reduce(jnp.add, terms))
-            if 1 <= s <= bx:
-                fiber = [fibers[number, s - 1, rows] for number in range(3)]
-            else:
-                fiber = fiber_of(*(cells[number, s, TOP + 8 * half : TOP + 8 * half + 8] for number in (1, 2)))
+            start = s * by + 8 * half
+            entries = [refined[k][start : start + 8] for k in range(parts)]
+            fiber = [fibers[number, s, rows] for number in range(3)]
             for number, value in enumerate(tensor_of(entries, fiber)):
                 conducts[number, s, TOP + 8 * half : TOP + 8 * half + 8] = value
             if 1 <= s <= bx:
                 out_potential[s - 1, rows] = stretch_of(entries, fiber)
-    rim_row = lax.rem(lax.broadcasted_iota(jnp.int32, (2 * bx, nz), 0), bx).astype(jnp.float32)
-    spot = (rim_row + 0.5) * (1.0 / RATIO) - 0.5
-    rim_weights = [jnp.maximum(1.0 - jnp.abs(spot - (q - 1.0)), 0.0) for q in range(3)]
-    entries = []
-    for k in range(parts):
-        at = tall * k + by
-        entries.append(
-            functools.reduce(
-                jnp.add, [rim_weights[q] * refined[q][at : at + 2 * bx] for q in range(3)]
-            )
-        )
+    start = (bx + 2) * by
+    entries = [refined[k][start : start + 2 * bx] for k in range(parts)]
+    rim_fiber = [rim_fibers[number] for number in range(3)]
     for number, value in enumerate(tensor_of(entries, rim_fiber)):
         for s in range(bx):
             conducts[number, s + 1, TOP - 1 : TOP] = value[s : s + 1]
@@ -454,11 +473,8 @@
         divergent = (
             (faces[i + 1] - faces[i]) + (upper - lower) + (face_z - pltpu.roll(face_z, 1, 1))
         )
-        voltage = middle[s]
-        resting = rest_in[i]
-        current = 8.0 * voltage * (voltage - 0.15) * (voltage - 1.0) + voltage * resting
-        current = current + 10.0 * jnp.maximum(out_potential[i] - 1.0, 0.0) * (voltage - 0.6)
-        out_potential[i] = voltage + 0.1 * (divergent - current)
+        extra = jnp.maximum(out_potential[i] - 1.0, 0.0) * (middle[s] - 0.6)
+        out_potential[i] = base[i] + 0.1 * divergent - extra
         copy = pltpu.make_async_copy(out_potential.at[i], next_potential.at[i], out_sem.at[i])
         copy.start()
         leaving.append(copy)
@@ -473,7 +489,7 @@
         bx, by, nz = potential.shape
         ex, ey, ez = slots.shape
         parts, count = deform.shape
-        assert ex == 1 and bx == RATIO and by % 8 == 0 and count % LANES == 0 and parts == 9
+        assert ex == 1 and bx == RATIO and by % 8 == 0 and count % LANES == 0 and parts == 9 and 4 < ey + 2 <= 8
         sizes = (bx, by, nz, ex, ey, ez, parts, count)
         blocks = count // LANES
         width = (ey + 2) * ez
@@ -482,13 +498,17 @@
         anywhere = pl.BlockSpec(memory_space=pl.ANY)
         in_vmem = pl.BlockSpec(memory_space=pltpu.VMEM)
         passed = (
-            pltpu.VMEM((3, bx + 2, by + 16, nz), f32),
+            pltpu.VMEM((bx + 2, by + 16, nz), f32),
+            pltpu.VMEM(recovery.shape, f32),
             pltpu.VMEM(recovery.shape, f32),
             pltpu.VMEM((3, down, 8 * blocks + 8, LANES), f32),
-            pltpu.VMEM((3, 3, ex, ey, ez), jnp.int32),
-            pltpu.VMEM((3, bx, by, nz), f32),
-            pltpu.VMEM((by + 8, width), f32),
+            pltpu.VMEM((3, LANES, width), jnp.bfloat16),
+            pltpu.VMEM((3, 1, width), jnp.int32),
+            pltpu.VMEM((3, bx + 2, by, nz), f32),
+            pltpu.VMEM((3, 2 * bx, nz), f32),
+            pltpu.VMEM(((bx + 2) * by + 2 * bx + 8, 48), jnp.bfloat16),
             pltpu.VMEM((width, nz), jnp.bfloat16),
+            pltpu.VMEM((8 * parts, nz), f32),
         )
         arrived = pl.pallas_call(
             functools.partial(exchange, across, down, sizes),
@@ -496,6 +516,9 @@
             in_specs=[pl.BlockSpec(memory_space=pltpu.MemorySpace.HBM)] * 5,
             out_specs=(in_vmem,) * len(passed),
             scratch_shapes=[
+                pltpu.VMEM((3, bx + 2, by + 16, nz), f32),
+                pltpu.VMEM(recovery.shape, f32),
+                pltpu.VMEM((3, 3, ex, ey, ez), jnp.int32),
                 pltpu.SemaphoreType.DMA((3 * down + 18,)),
                 pltpu.SemaphoreType.DMA((3 * down,)),
                 pltpu.SemaphoreType.DMA((18,)),
@@ -511,9 +534,7 @@
             in_specs=[in_vmem] * len(passed),
             out_specs=(anywhere,) * 2,
             scratch_shapes=[
-                pltpu.VMEM((bx + 2, by + 16, nz), f32),
                 pltpu.VMEM((6, bx + 2, by + 16, nz), f32),
-                pltpu.VMEM((bx, by, nz), f32),
                 pltpu.VMEM((bx, by, nz), f32),
                 pltpu.SemaphoreType.DMA((bx + 1,)),
             ],

time: 11.4 us -> 11.5 us (level)
    pallas_call x1, Pallas kernels: 8.08 us -> 8.39 us  [local(): pl.pallas_call(functools.partial(exchange, across, down, sizes), out_shap...]
    pallas_call x1, Pallas kernels: 2.55 us -> 2.33 us  [local(): pl.pallas_call(functools.partial(compute, across, down, sizes), out_shape...]
where the time goes in v3:
time: 11.5 us; the launch traced here: 11.4 us
  Pallas kernels  10.7 us (93%)
  between operations  0.64 us (6%)
    pallas_call x1, Pallas kernels, local(): pl.pallas_call(functools.partial(exchange, across, down, sizes), out_shap...  8.39 us
    pallas_call x1, Pallas kernels, local(): pl.pallas_call(functools.partial(compute, across, down, sizes), out_shape...  2.33 us

profile of v3, /device:TPU:1, one launch (start us, length us, event | category | flops | bytes accessed | tf_op | source)
XLA Modules:
  0.0 11.4 jit_solution(11618665806780577267)
XLA Ops:
  0.6 8.4 %shard_map.68 = (f32[6,32,256]{2,1,0:T(8,128)S(1)}, f32[4,16,256]{2,1,0:T(8,128)S(1)}, f32[4,16,256]{2,1,0:T(8,128)S(1)}, f32[3,4,24,128]{3,2,1,0:T(8,128)S(1)},...) custom-call(f32[4,16,256]{2,1,0:T(8,128)} %potential.1, ...), custom_call_target="tpu_custom_call" | custom-call | tf_op jit(solution)/shard_map/pallas_call | solution.py:513
  9.0 2.3 %shard_map.69 = (f32[4,16,256]{2,1,0:T(8,128)}, f32[4,16,256]{2,1,0:T(8,128)}) custom-call(f32[6,32,256]{2,1,0:T(8,128)S(1)} %get-tuple-element.13.volts, f32[4,16,256]{2,1,0:T(8,128)S(1)} %get-tuple-element.14.base, f32[4,16,256]{2,1,0:T(8,128)S(1)} %get-tuple-element.15.new_recovery, f32[3,4,24,128]{3,2,1,0:T(8,128)S(1)} %get-tuple-element.16.held, ...), custom_call_target="tpu_custom_call" | custom-call | tf_op jit(solution)/shard_map/pallas_call | solution.py:531
